TPU v7x, 32 devices: a whole 2x2x4 slice. The times are simulated.
32 devices in a mesh: px: 8 (over z, x), py: 4 (over y, core).
Axes of the slice: x: 2, y: 2, z: 4, core: 2. Of those that a mesh axis runs over, the one named last changes fastest.
Arguments:
- potential: float32 [256, 256, 256], P(('px', 'py')), may hold values from 0 to 1
- recovery: float32 [256, 256, 256], P(('px', 'py')), may hold values from 0 to 2
- stimulus: float32 [256, 256, 256], P(('px', 'py')), may hold values from -8 to 8
- conductivity: float32 [256, 256, 256], P('px', 'py'), may hold values from 0.2 to 5
Outputs:
- potential_next: float32 [256, 256, 256], P(('px', 'py'))
- recovery_next: float32 [256, 256, 256], P(('px', 'py'))
All inputs are finite; a program needn't handle non-finite values.
Results may differ from a plain program's by a relative error of at most 0.0003.
Values sent between devices are 32-bit elements; how exact they have to be, the bound alone decides.
A program may use at most 128 MiB of HBM per device.

v0:
```python
import math

import jax
import jax.numpy as jnp
import numpy as np
from jax import lax
from jax.experimental import pallas as pl
from jax.experimental.pallas import tpu as pltpu
from jax.sharding import PartitionSpec as P

ITERS = 4

mass_rate = 0.01
excite_gain = 8.0
threshold = 0.15
base_rate = 0.002
rate_slope = 0.2
rate_shift = 0.3
time_step = 0.1
AXES = ("px", "py")


def cas_table(length):
    steps = np.arange(length)
    angle = 2.0 * math.pi / length * (steps[:, None] * steps[None, :] % length)
    return np.cos(angle) + np.sin(angle)


def wave_term(length):
    return 2.0 - 2.0 * np.cos(2.0 * math.pi / length * np.arange(length))


def mode_tables(length_y, length_z):
    shift = mass_rate + wave_term(length_y)[:, None] + wave_term(length_z)[None, :]
    root = np.sqrt(shift * (4.0 + shift))
    rho = 2.0 / (2.0 + shift + root)
    scale = 1.0 / (root * length_y * length_z)
    return rho, scale


def local(potential, recovery, stimulus, conductivity):
    devices = lax.axis_size("px") * lax.axis_size("py")
    me = lax.axis_index(AXES)
    rows, length_y, length_z = potential.shape
    length_x = rows * devices
    forth = [(i, (i + 1) % devices) for i in range(devices)]
    back = [((i + 1) % devices, i) for i in range(devices)]
    drive = (
        excite_gain * potential * (potential - threshold) * (1.0 - potential) - potential * recovery
    )
    v_star = potential + time_step * (drive + stimulus)
    rate = base_rate + rate_slope * recovery / (potential + rate_shift)
    recovery_next = recovery + time_step * rate * (
        -recovery - excite_gain * potential * (potential - threshold - 1.0)
    )
    cond = lax.all_to_all(conductivity, "py", split_axis=0, concat_axis=1, tiled=True)

    def above(field):
        return lax.ppermute(field[:1], AXES, back)

    def below(field):
        return lax.ppermute(field[-1:], AXES, forth)

    cond_x = jnp.concatenate([below(cond), cond, above(cond)], 0)
    face_x = 0.5 * (cond_x[1:] + cond_x[:-1])
    face_y = 0.5 * (cond + jnp.roll(cond, -1, 1))
    face_z = 0.5 * (cond + jnp.roll(cond, -1, 2))

    def faces(field):
        padded = jnp.concatenate([below(field), field, above(field)], 0)
        flow_x = face_x * (padded[:-1] - padded[1:])
        flow_y = face_y * (field - jnp.roll(field, -1, 1))
        flow_z = face_z * (field - jnp.roll(field, -1, 2))
        return (
            (flow_x[1:] - flow_x[:-1])
            + (flow_y - jnp.roll(flow_y, 1, 1))
            + (flow_z - jnp.roll(flow_z, 1, 2))
        )

    rho64, scale64 = mode_tables(length_y, length_z)
    rho = jnp.asarray(rho64, jnp.float32)
    scale = jnp.asarray(scale64, jnp.float32)
    cas_y = jnp.asarray(cas_table(length_y), jnp.float32)
    cas_z = jnp.asarray(cas_table(length_z), jnp.float32)
    step_log = jnp.asarray(rows * np.log(rho64), jnp.float32)
    closing = jnp.asarray(1.0 / (1.0 - rho64**length_x), jnp.float32)
    part = length_y // devices
    step_log = lax.dynamic_slice_in_dim(step_log, me * part, part, 0)
    closing = lax.dynamic_slice_in_dim(closing, me * part, part, 0)
    order = np.arange(devices)
    gap = jnp.asarray((order[:, None] - 1 - order[None, :]) % devices, jnp.float32)

    def both(field):
        field = jnp.einsum("xyz,zk->xyk", field, cas_z, precision=lax.Precision.HIGH)
        return jnp.einsum("xyk,yq->xqk", field, cas_y, precision=lax.Precision.HIGH)

    def apply_inverse(residual):
        spectrum = both(residual)
        head = spectrum[rows - 1]
        tail = spectrum[0]
        for i in range(1, rows):
            head = head + rho**i * spectrum[rows - 1 - i]
            tail = tail + rho**i * spectrum[i]
        ends = jnp.stack([head, tail])[None]
        ends = lax.all_to_all(ends, AXES, split_axis=2, concat_axis=0, tiled=True)
        power = jnp.exp(gap[:, :, None, None] * step_log) * closing
        left = jnp.sum(power * ends[None, :, 0], 1)
        right = jnp.sum(jnp.swapaxes(power, 0, 1) * ends[None, :, 1], 1)
        carry = jnp.stack([left, right], 1)
        carry = lax.all_to_all(carry, AXES, split_axis=0, concat_axis=2, tiled=True)
        forward, backward = [None] * rows, [None] * rows
        value = carry[0, 0]
        for i in range(rows):
            value = spectrum[i] + rho * value
            forward[i] = value
        value = carry[0, 1]
        for i in reversed(range(rows)):
            backward[i] = rho * value
            value = spectrum[i] + backward[i]
        return both(jnp.stack([scale * (f + b) for f, b in zip(forward, backward)]))

    field = v_star
    residual = -faces(v_star)
    direction = image = gamma = alpha = None
    for step in range(ITERS):
        precond = apply_inverse(residual)
        applied = mass_rate * precond + faces(precond)
        sums = jnp.stack([jnp.sum(residual * precond), jnp.sum(applied * precond)])
        sums = jnp.sum(lax.all_gather(jnp.broadcast_to(sums[:, None], (2, 128)), AXES), 0)
        gamma_next, delta = sums[0, 0], sums[1, 0]
        if step == 0:
            alpha = gamma_next / delta
            direction, image = precond, applied
        else:
            beta = gamma_next / gamma
            alpha = gamma_next / (delta - beta * gamma_next / alpha)
            direction = precond + beta * direction
            image = applied + beta * image
        gamma = gamma_next
        field = field + alpha * direction
        residual = residual - alpha * image
    return (field, recovery_next)


def split(table):
    high = table.astype(jnp.bfloat16)
    low = (table - high.astype(np.float64)).astype(jnp.bfloat16)
    return jnp.asarray(high), jnp.asarray(low)


def parts_of(block):
    high = block.astype(jnp.bfloat16)
    return high, (block - high.astype(jnp.float32)).astype(jnp.bfloat16)


def product(left, right):
    def dot(a, b):
        return jnp.dot(a, b, preferred_element_type=jnp.float32)

    return dot(left[0], right[1]) + dot(left[1], right[0]) + dot(left[0], right[0])


def kernel(
    v_ref, cond_in, yh_ref, yl_ref, zh_ref, zl_ref, rho_ref, scale_ref, sigma_ref, close_ref,
    u_ref,
    cond, face_x, face_y, face_z, res, dire, imag, z_ref, w_ref, spec, back_ref, power,
    ends, recv, sol, carry, mine, gath,
    c_send, c_recv, h_send, h_recv, e_send, e_recv, s_send, s_recv, g_send, g_recv,
):
    count_y = lax.axis_size("py")
    devices = lax.axis_size("px") * count_y
    my_y = lax.axis_index("py")
    me = lax.axis_index("px") * count_y + my_y
    rows, length_y, length_z = v_ref.shape
    part = length_y // devices
    wide_y = cond_in.shape[1]
    mesh_type = pl.DeviceIdType.MESH

    def device(index):
        return (index // count_y, index % count_y)

    def strip(index):
        return pl.ds(pl.multiple_of(index * part, part), part)

    def halo(buffer, base):
        left = (me + devices - 1) % devices
        right = (me + 1) % devices
        return (
            pltpu.make_async_remote_copy(
                buffer.at[1], buffer.at[rows + 1], h_send.at[base], h_recv.at[base],
                device_id=device(left), device_id_type=mesh_type,
            ),
            pltpu.make_async_remote_copy(
                buffer.at[rows], buffer.at[0], h_send.at[base + 1], h_recv.at[base + 1],
                device_id=device(right), device_id_type=mesh_type,
            ),
        )

    def start_all(make, count):
        def begin(k, _):
            make(k).start()
            return 0

        lax.fori_loop(1, count, begin, 0)

    def wait_all(make, count):
        def finish(k, _):
            make(k).wait()
            return 0

        lax.fori_loop(1, count, finish, 0)

    def cond_copy(k):
        other = (my_y + k) % count_y
        return pltpu.make_async_remote_copy(
            cond_in.at[pl.ds(other * rows, rows)],
            cond.at[pl.ds(1, rows), pl.ds(pl.multiple_of(my_y * wide_y, 8), wide_y), :],
            c_send.at[k], c_recv.at[k],
            device_id=(lax.axis_index("px"), other), device_id_type=mesh_type,
        )

    def ends_copy(k):
        other = (me + k) % devices
        return pltpu.make_async_remote_copy(
            ends.at[:, strip(other), :], recv.at[me], e_send.at[k], e_recv.at[k],
            device_id=device(other), device_id_type=mesh_type,
        )

    def carry_copy(k):
        other = (me + k) % devices
        return pltpu.make_async_remote_copy(
            sol.at[other], carry.at[:, strip(me), :], s_send.at[k], s_recv.at[k],
            device_id=device(other), device_id_type=mesh_type,
        )

    def gath_copy(k):
        other = (me + k) % devices
        return pltpu.make_async_remote_copy(
            mine, gath.at[me], g_send.at[k], g_recv.at[k],
            device_id=device(other), device_id_type=mesh_type,
        )

    def stencil(k, _):
        i = (k + 1) % rows
        here = z_ref[i + 1]
        total = face_x[i + 1] * (here - z_ref[i + 2]) - face_x[i] * (z_ref[i] - here)
        flow = face_y[i] * (here - pltpu.roll(here, length_y - 1, 0))
        total = total + (flow - pltpu.roll(flow, 1, 0))
        flow = face_z[i] * (here - pltpu.roll(here, length_z - 1, 1))
        w_ref[i] = total + (flow - pltpu.roll(flow, 1, 1))
        return 0

    start_all(cond_copy, count_y)
    for i in range(rows):
        z_ref[i + 1] = v_ref[i]
        u_ref[i] = v_ref[i]
    field_halo = halo(z_ref, 0)
    for copy in field_halo:
        copy.start()
    cond[pl.ds(1, rows), pl.ds(pl.multiple_of(my_y * wide_y, 8), wide_y), :] = cond_in[
        pl.ds(my_y * rows, rows)
    ]
    wait_all(cond_copy, count_y)
    cond_halo = halo(cond, 2)
    for copy in cond_halo:
        copy.start()

    def faces(i, _):
        here = cond[i + 1]
        face_y[i] = 0.5 * (here + pltpu.roll(here, length_y - 1, 0))
        face_z[i] = 0.5 * (here + pltpu.roll(here, length_z - 1, 1))
        return 0

    lax.fori_loop(0, rows, faces, 0)
    for copy in cond_halo + field_halo:
        copy.wait()

    def faces_along(i, _):
        face_x[i] = 0.5 * (cond[i] + cond[i + 1])
        return 0

    lax.fori_loop(0, rows + 1, faces_along, 0)
    lax.fori_loop(0, rows, stencil, 0)

    def first(i, _):
        res[i] = -w_ref[i]
        dire[i] = jnp.zeros((length_y, length_z), jnp.float32)
        imag[i] = jnp.zeros((length_y, length_z), jnp.float32)
        return 0

    lax.fori_loop(0, rows, first, 0)

    def iteration(step, scalars):
        gamma, alpha = scalars
        ends[...] = jnp.zeros_like(ends)
        power[...] = jnp.ones_like(power)

        def ahead(i, _):
            block = product(parts_of(res[i]), (zh_ref[...], zl_ref[...]))
            block = product((yh_ref[...], yl_ref[...]), parts_of(block))
            spec[i] = block
            rho = rho_ref[...]
            ends[0] = block + rho * ends[0]
            ends[1] = ends[1] + power[...] * block
            power[...] = power[...] * rho
            return 0

        lax.fori_loop(0, rows, ahead, 0)
        start_all(ends_copy, devices)
        recv[me] = ends[:, strip(me), :]
        wait_all(ends_copy, devices)

        sigma = sigma_ref[strip(me), :]
        close = close_ref[strip(me), :]
        zero = jnp.zeros_like(sigma)

        def sums(b, pair):
            return (
                recv[b, 0] + sigma * pair[0],
                recv[devices - 1 - b, 1] + sigma * pair[1],
            )

        pair = lax.fori_loop(0, devices, sums, (zero, zero), unroll=4)

        def place(b, pair):
            c = devices - 1 - b
            sol[b, 0] = pair[0]
            sol[c, 1] = pair[1]
            return sums(b, pair)

        lax.fori_loop(0, devices, place, (pair[0] * close, pair[1] * close), unroll=4)
        start_all(carry_copy, devices)
        carry[:, strip(me), :] = sol[me]
        wait_all(carry_copy, devices)

        def behind(j, _):
            i = rows - 1 - j
            value = rho_ref[...] * carry[1]
            back_ref[i] = value
            carry[1] = spec[i] + value
            return 0

        lax.fori_loop(0, rows, behind, 0)

        def inverse(i, _):
            value = spec[i] + rho_ref[...] * carry[0]
            carry[0] = value
            value = scale_ref[...] * (value + back_ref[i])
            value = product((yh_ref[...], yl_ref[...]), parts_of(value))
            z_ref[i + 1] = product(parts_of(value), (zh_ref[...], zl_ref[...]))
            return 0

        lax.fori_loop(0, rows, inverse, 0)
        copies = halo(z_ref, 0)
        for copy in copies:
            copy.start()
        lax.fori_loop(0, rows - 2, stencil, 0)
        for copy in copies:
            copy.wait()
        lax.fori_loop(rows - 2, rows, stencil, 0)

        mine[...] = jnp.zeros_like(mine)

        def fold(value):
            value = jnp.sum(value.reshape(length_y // 8, 8, length_z), 0)
            return sum(value[:, c : c + 128] for c in range(0, length_z, 128))

        def dots(i, _):
            z = z_ref[i + 1]
            applied = mass_rate * z + w_ref[i]
            w_ref[i] = applied
            mine[0] = mine[0] + fold(z * res[i])
            mine[1] = mine[1] + fold(z * applied)
            return 0

        lax.fori_loop(0, rows, dots, 0)
        start_all(gath_copy, devices)
        gath[me] = mine[...]
        wait_all(gath_copy, devices)
        total = jnp.sum(gath[...], 0)
        gamma_next = jnp.sum(total[0], keepdims=True)
        delta = jnp.sum(total[1], keepdims=True)
        beta = jnp.where(step == 0, 0.0, gamma_next / gamma)
        alpha_next = gamma_next / (delta - beta * gamma_next / alpha)

        def update(i, _):
            direction = z_ref[i + 1] + beta * dire[i]
            image = w_ref[i] + beta * imag[i]
            dire[i] = direction
            imag[i] = image
            u_ref[i] = u_ref[i] + alpha_next * direction
            res[i] = res[i] - alpha_next * image
            return 0

        lax.fori_loop(0, rows, update, 0)
        return gamma_next, alpha_next

    one = jnp.ones((1, 1), jnp.float32)
    lax.fori_loop(0, ITERS, iteration, (one, one))


def fused(potential, recovery, stimulus, conductivity):
    devices = lax.axis_size("px") * lax.axis_size("py")
    rows, length_y, length_z = potential.shape
    part = length_y // devices
    if part % 8 or length_z % 128 or conductivity.shape[1] % 8:
        return local(potential, recovery, stimulus, conductivity)
    drive = (
        excite_gain * potential * (potential - threshold) * (1.0 - potential) - potential * recovery
    )
    v_star = potential + time_step * (drive + stimulus)
    rate = base_rate + rate_slope * recovery / (potential + rate_shift)
    recovery_next = recovery + time_step * rate * (
        -recovery - excite_gain * potential * (potential - threshold - 1.0)
    )
    rho, scale = mode_tables(length_y, length_z)
    tables = split(cas_table(length_y)) + split(cas_table(length_z))
    tables += tuple(
        jnp.asarray(table, jnp.float32)
        for table in (rho, scale, rho**rows, 1.0 / (1.0 - rho ** (rows * devices)))
    )
    plane = (length_y, length_z)
    whole = (rows,) + plane

    def vmem(shape):
        return pltpu.VMEM(shape, jnp.float32)

    dma = pltpu.SemaphoreType.DMA
    padded = (rows + 2,) + plane
    slots = (devices, 2, part, length_z)
    field = pl.pallas_call(
        kernel,
        out_shape=jax.ShapeDtypeStruct(whole, jnp.float32),
        in_specs=[pl.BlockSpec(memory_space=pltpu.VMEM)] * 10,
        out_specs=pl.BlockSpec(memory_space=pltpu.VMEM),
        scratch_shapes=[
            vmem(padded), vmem((rows + 1,) + plane), vmem(whole), vmem(whole),
            vmem(whole), vmem(whole), vmem(whole), vmem(padded), vmem(whole),
            vmem(whole), vmem(whole), vmem(plane),
            vmem((2,) + plane), vmem(slots), vmem(slots), vmem((2,) + plane),
            vmem((2, 8, 128)), vmem((devices, 2, 8, 128)),
            dma((devices,)), dma((devices,)), dma((4,)), dma((4,)),
            dma((devices,)), dma((devices,)), dma((devices,)), dma((devices,)),
            dma((devices,)), dma((devices,)),
        ],
        compiler_params=pltpu.CompilerParams(
            has_side_effects=True, vmem_limit_bytes=56 * 1024 * 1024
        ),
    )(v_star, conductivity, *tables)
    return (field, recovery_next)


def solution(mesh):
    in_specs = (
        P(AXES, None, None),
        P(AXES, None, None),
        P(AXES, None, None),
        P("px", "py", None),
    )
    out_specs = (P(AXES, None, None), P(AXES, None, None))
    return jax.shard_map(fused, mesh=mesh, in_specs=in_specs, out_specs=out_specs, check_vma=False)
```

profile of v0, /device:TPU:0, one launch (start us, length us, event | category | flops | bytes accessed | tf_op | source)
XLA Modules:
  0.0 277.0 jit_solution(11014324677663106630)
XLA Ops:
  0.6 4.9 %multiply_add_fusion = (f32[8,256,256]{2,1,0:T(8,128)}, f32[8,256,256]{2,1,0:T(8,128)}) fusion(f32[8,256,256]{2,1,0:T(8,128)} %param.13, f32[8,256,256]{2,1,0:T(8,128)} %param.12, f32[8,256,256]{2,1,0:T(8,128)} %param.14), kind=kLoop, calls=%fused_computation | loop fusion | flops 11010048 | bytes 10485760 | tf_op jit(solution)/shard_map/add | solution.py:413
  5.5 0.8 jit_solution_.3.close_ref
  6.3 267.6 %shard_map.131 = f32[8,256,256]{2,1,0:T(8,128)} custom-call(f32[8,256,256]{2,1,0:T(8,128)} %get-tuple-element.3.v_ref, f32[32,64,256]{2,1,0:T(8,128)} %cond_in.1, bf16[256,256]{1,0:T(8,128)(2,1)} %constant.30.clone.yh_ref.zh_ref, bf16[256,256]{1,0:T(8,128)(2,1)} %constant.31.clone.yl_ref.zl_ref, bf16[256,256]{1,0:T(8,128)(2,1)} %constant.30.clone.yh_ref.zh_ref, ...), custom_call_target="tpu_custom_call" | custom-call | tf_op jit(solution)/shard_map/pallas_call | solution.py:431
  273.9 3.0 %copy.15 = f32[8,256,256]{2,1,0:T(8,128)} copy(f32[8,256,256]{2,1,0:T(8,128)} %shard_map.131) | data formatting | bytes 4194304
where the time goes:
time: 277 us
  Pallas kernels  268 us (97%)
  other arithmetic  4.88 us (2%)
  local copies, waits for them, and re-layouts  3.8 us (1%)
    pallas_call x1, Pallas kernels, fused(): pl.pallas_call(kernel, out_shape=jax.ShapeDtypeStruct(whole, jnp.float32)...  268 us

commit v1 on v0

--- a/solution.py
+++ b/solution.py
@@ -17,6 +17,8 @@
 rate_slope = 0.2
 rate_shift = 0.3
 time_step = 0.1
+nodes = (2.6, 1.0, 4.0)
+pivot_floor = 1e-6
 AXES = ("px", "py")
 
 
@@ -161,18 +163,24 @@
 
 
 def kernel(
-    v_ref, cond_in, yh_ref, yl_ref, zh_ref, zl_ref, rho_ref, scale_ref, sigma_ref, close_ref,
+    v_ref, cond_in, yh_ref, yl_ref, zh_ref, zl_ref, rho_ref, scale_ref, sigma_ref, pair_ref,
+    close_ref,
     u_ref,
-    cond, face_x, face_y, face_z, res, dire, imag, z_ref, w_ref, spec, back_ref, power,
-    ends, recv, sol, carry, mine, gath,
-    c_send, c_recv, h_send, h_recv, e_send, e_recv, s_send, s_recv, g_send, g_recv,
+    cond, face_x, face_y, face_z, zs, res, first, imag, spec, mode_h, mode_l,
+    out, both_ends, chip, recv, sol, car, back, carry, dots, mine, gath,
+    c_send, c_recv, h_send, h_recv, p_send, p_recv, e_send, e_recv, s_send, s_recv,
+    g_send, g_recv,
 ):
     count_y = lax.axis_size("py")
     devices = lax.axis_size("px") * count_y
+    chips = devices // 2
     my_y = lax.axis_index("py")
     me = lax.axis_index("px") * count_y + my_y
+    core = me % 2
+    my_chip = me // 2
     rows, length_y, length_z = v_ref.shape
-    part = length_y // devices
+    half = length_y // 2
+    part = half // chips
     wide_y = cond_in.shape[1]
     mesh_type = pl.DeviceIdType.MESH
 
@@ -181,18 +189,19 @@
 
     def strip(index):
         return pl.ds(pl.multiple_of(index * part, part), part)
+
+    def remote(source, target, send, recv_sem, index):
+        return pltpu.make_async_remote_copy(
+            source, target, send, recv_sem, device_id=device(index), device_id_type=mesh_type
+        )
 
     def halo(buffer, base):
         left = (me + devices - 1) % devices
         right = (me + 1) % devices
         return (
-            pltpu.make_async_remote_copy(
-                buffer.at[1], buffer.at[rows + 1], h_send.at[base], h_recv.at[base],
-                device_id=device(left), device_id_type=mesh_type,
-            ),
-            pltpu.make_async_remote_copy(
-                buffer.at[rows], buffer.at[0], h_send.at[base + 1], h_recv.at[base + 1],
-                device_id=device(right), device_id_type=mesh_type,
+            remote(buffer.at[1], buffer.at[rows + 1], h_send.at[base], h_recv.at[base], left),
+            remote(
+                buffer.at[rows], buffer.at[0], h_send.at[base + 1], h_recv.at[base + 1], right
             ),
         )
 
@@ -220,46 +229,51 @@
         )
 
     def ends_copy(k):
-        other = (me + k) % devices
-        return pltpu.make_async_remote_copy(
-            ends.at[:, strip(other), :], recv.at[me], e_send.at[k], e_recv.at[k],
-            device_id=device(other), device_id_type=mesh_type,
+        other = (my_chip + k) % chips
+        return remote(
+            chip.at[:, strip(other), :], recv.at[my_chip], e_send.at[k], e_recv.at[k],
+            2 * other + core,
         )
 
     def carry_copy(k):
-        other = (me + k) % devices
-        return pltpu.make_async_remote_copy(
-            sol.at[other], carry.at[:, strip(me), :], s_send.at[k], s_recv.at[k],
-            device_id=device(other), device_id_type=mesh_type,
+        other = (my_chip + k) % chips
+        return remote(
+            sol.at[other], car.at[:, strip(my_chip), :], s_send.at[k], s_recv.at[k],
+            2 * other + core,
         )
 
     def gath_copy(k):
-        other = (me + k) % devices
-        return pltpu.make_async_remote_copy(
-            mine, gath.at[me], g_send.at[k], g_recv.at[k],
-            device_id=device(other), device_id_type=mesh_type,
-        )
-
-    def stencil(k, _):
-        i = (k + 1) % rows
-        here = z_ref[i + 1]
-        total = face_x[i + 1] * (here - z_ref[i + 2]) - face_x[i] * (z_ref[i] - here)
+        return remote(mine, gath.at[me], g_send.at[k], g_recv.at[k], (me + k) % devices)
+
+    partner = me + 1 - 2 * core
+    pair_ends = remote(out, both_ends.at[core], p_send.at[0], p_recv.at[0], partner)
+    pair_carry = remote(back, carry.at[core], p_send.at[1], p_recv.at[1], partner)
+
+    def flux(field, i):
+        here = field[i + 1]
+        total = face_x[i + 1] * (here - field[i + 2]) - face_x[i] * (field[i] - here)
         flow = face_y[i] * (here - pltpu.roll(here, length_y - 1, 0))
         total = total + (flow - pltpu.roll(flow, 1, 0))
         flow = face_z[i] * (here - pltpu.roll(here, length_z - 1, 1))
-        w_ref[i] = total + (flow - pltpu.roll(flow, 1, 1))
-        return 0
+        return here, total + (flow - pltpu.roll(flow, 1, 1))
 
     start_all(cond_copy, count_y)
+    start = zs.at[0]
     for i in range(rows):
-        z_ref[i + 1] = v_ref[i]
-        u_ref[i] = v_ref[i]
-    field_halo = halo(z_ref, 0)
+        start[i + 1] = v_ref[i]
+    field_halo = halo(start, 0)
     for copy in field_halo:
         copy.start()
     cond[pl.ds(1, rows), pl.ds(pl.multiple_of(my_y * wide_y, 8), wide_y), :] = cond_in[
         pl.ds(my_y * rows, rows)
     ]
+
+    def clear(i, _):
+        for k in range(1, ITERS):
+            zs[k, i + 1] = jnp.zeros((length_y, length_z), jnp.float32)
+        return 0
+
+    lax.fori_loop(0, rows, clear, 0)
     wait_all(cond_copy, count_y)
     cond_halo = halo(cond, 2)
     for copy in cond_halo:
@@ -280,130 +294,236 @@
         return 0
 
     lax.fori_loop(0, rows + 1, faces_along, 0)
-    lax.fori_loop(0, rows, stencil, 0)
-
-    def first(i, _):
-        res[i] = -w_ref[i]
-        dire[i] = jnp.zeros((length_y, length_z), jnp.float32)
-        imag[i] = jnp.zeros((length_y, length_z), jnp.float32)
+
+    def begin(i, _):
+        _, total = flux(start, i)
+        first[i] = -total
+        res[i] = -total
         return 0
 
-    lax.fori_loop(0, rows, first, 0)
-
-    def iteration(step, scalars):
-        gamma, alpha = scalars
-        ends[...] = jnp.zeros_like(ends)
-        power[...] = jnp.ones_like(power)
-
-        def ahead(i, _):
-            block = product(parts_of(res[i]), (zh_ref[...], zl_ref[...]))
-            block = product((yh_ref[...], yl_ref[...]), parts_of(block))
-            spec[i] = block
-            rho = rho_ref[...]
-            ends[0] = block + rho * ends[0]
-            ends[1] = ends[1] + power[...] * block
-            power[...] = power[...] * rho
-            return 0
-
-        lax.fori_loop(0, rows, ahead, 0)
-        start_all(ends_copy, devices)
-        recv[me] = ends[:, strip(me), :]
-        wait_all(ends_copy, devices)
-
-        sigma = sigma_ref[strip(me), :]
-        close = close_ref[strip(me), :]
+    lax.fori_loop(0, rows, begin, 0)
+
+    def products(step):
+        block = 8
+        per = length_y // block
+
+        def body(t, sums):
+            i = t // per
+            at = pl.ds(pl.multiple_of((t % per) * block, block), block)
+            image = imag[i, at, :]
+            fresh = [zs[j, i + 1, at, :] for j in range(ITERS)]
+            sums = [total + z * image for total, z in zip(sums, fresh)] + [
+                sums[ITERS] + zs[step, i + 1, at, :] * first[i, at, :]
+            ]
+            return tuple(sums)
+
+        zero = jnp.zeros((block, length_z), jnp.float32)
+        sums = lax.fori_loop(0, rows * per, body, (zero,) * (ITERS + 1), unroll=4)
+        for m, total in enumerate(sums):
+            dots[step, m] = sum(total[:, c : c + 128] for c in range(0, length_z, 128))
+
+    def block_ends(where, side, target, block=8):
+        def body(b, _):
+            low = pl.multiple_of(b * block, block)
+            at = pl.ds(pl.multiple_of(side * half + low, block), block)
+            rho = rho_ref[at, :]
+            planes = [spec[i, at, :] for i in range(rows)]
+            head, tail = planes[0], planes[rows - 1]
+            for i in range(1, rows):
+                head = planes[i] + rho * head
+                tail = planes[rows - 1 - i] + rho * tail
+            target[0, pl.ds(low, block), :] = head
+            target[1, pl.ds(low, block), :] = tail
+            return 0
+
+        lax.fori_loop(0, half // block, body, 0, unroll=2)
+
+    def chip_ends(block=8):
+        def body(b, _):
+            low = pl.multiple_of(b * block, block)
+            at = pl.ds(low, block)
+            sigma = sigma_ref[pl.ds(pl.multiple_of(core * half + low, block), block), :]
+            chip[0, at, :] = both_ends[1, 0, at, :] + sigma * both_ends[0, 0, at, :]
+            chip[1, at, :] = both_ends[0, 1, at, :] + sigma * both_ends[1, 1, at, :]
+            return 0
+
+        lax.fori_loop(0, half // block, body, 0, unroll=4)
+
+    def core_carries(block=8):
+        def body(b, _):
+            low = pl.multiple_of(b * block, block)
+            at = pl.ds(low, block)
+            sigma = sigma_ref[pl.ds(pl.multiple_of(core * half + low, block), block), :]
+            left, right = car[0, at, :], car[1, at, :]
+            after = both_ends[1, 1, at, :] + sigma * right
+            before = both_ends[0, 0, at, :] + sigma * left
+            carry[core, 0, at, :] = jnp.where(core == 0, left, before)
+            carry[core, 1, at, :] = jnp.where(core == 0, after, right)
+            back[0, at, :] = jnp.where(core == 0, before, left)
+            back[1, at, :] = jnp.where(core == 0, right, after)
+            return 0
+
+        lax.fori_loop(0, half // block, body, 0, unroll=4)
+
+    def recur(side, block=16, wide=128):
+        def body(b, _):
+            low = pl.multiple_of(b * block, block)
+            at = pl.ds(pl.multiple_of(side * half + low, block), block)
+            for c in range(0, length_z, wide):
+                cut = slice(c, c + wide)
+                rho = rho_ref[at, cut]
+                scale = scale_ref[at, cut]
+                left = carry[side, 0, pl.ds(low, block), cut]
+                right = carry[side, 1, pl.ds(low, block), cut]
+                planes = [spec[i, at, cut] for i in range(rows)]
+                ahead = [None] * rows
+                value = right
+                for i in reversed(range(rows)):
+                    ahead[i] = rho * value
+                    value = planes[i] + ahead[i]
+                modes = [left + rho * value]
+                value = left
+                for i in range(rows):
+                    value = planes[i] + rho * value
+                    modes.append(value + ahead[i])
+                modes.append(right + rho * value)
+                for i, mode in enumerate(modes):
+                    mode_h[i, at, cut], mode_l[i, at, cut] = parts_of(scale * mode)
+            return 0
+
+        lax.fori_loop(0, half // block, body, 0)
+
+    def solve():
+        own = pl.ds(pl.multiple_of(core * half + my_chip * part, part), part)
+        sigma = pair_ref[own, :]
+        close = close_ref[own, :]
         zero = jnp.zeros_like(sigma)
 
         def sums(b, pair):
             return (
                 recv[b, 0] + sigma * pair[0],
-                recv[devices - 1 - b, 1] + sigma * pair[1],
+                recv[chips - 1 - b, 1] + sigma * pair[1],
             )
 
-        pair = lax.fori_loop(0, devices, sums, (zero, zero), unroll=4)
+        pair = lax.fori_loop(0, chips, sums, (zero, zero), unroll=4)
 
         def place(b, pair):
-            c = devices - 1 - b
             sol[b, 0] = pair[0]
-            sol[c, 1] = pair[1]
+            sol[chips - 1 - b, 1] = pair[1]
             return sums(b, pair)
 
-        lax.fori_loop(0, devices, place, (pair[0] * close, pair[1] * close), unroll=4)
-        start_all(carry_copy, devices)
-        carry[:, strip(me), :] = sol[me]
-        wait_all(carry_copy, devices)
-
-        def behind(j, _):
-            i = rows - 1 - j
-            value = rho_ref[...] * carry[1]
-            back_ref[i] = value
-            carry[1] = spec[i] + value
-            return 0
-
-        lax.fori_loop(0, rows, behind, 0)
+        lax.fori_loop(0, chips, place, (pair[0] * close, pair[1] * close), unroll=4)
+
+    def iteration(step, _):
+        def ahead(i, _):
+            block = product(parts_of(res[i]), (zh_ref[...], zl_ref[...]))
+            spec[i] = product((yh_ref[...], yl_ref[...]), parts_of(block))
+            return 0
+
+        lax.fori_loop(0, rows, ahead, 0)
+        block_ends(spec, 1 - core, out)
+        pair_ends.start()
+        block_ends(spec, core, both_ends.at[core])
+        pair_ends.wait()
+        chip_ends()
+        start_all(ends_copy, chips)
+        recv[my_chip] = chip[:, strip(my_chip), :]
+
+        @pl.when(step > 0)
+        def _():
+            products(step - 1)
+
+        wait_all(ends_copy, chips)
+        solve()
+        start_all(carry_copy, chips)
+        car[:, strip(my_chip), :] = sol[my_chip]
+        wait_all(carry_copy, chips)
+        core_carries()
+        pair_carry.start()
+        recur(core)
+        pair_carry.wait()
+        recur(1 - core)
 
         def inverse(i, _):
-            value = spec[i] + rho_ref[...] * carry[0]
-            carry[0] = value
-            value = scale_ref[...] * (value + back_ref[i])
-            value = product((yh_ref[...], yl_ref[...]), parts_of(value))
-            z_ref[i + 1] = product(parts_of(value), (zh_ref[...], zl_ref[...]))
-            return 0
-
-        lax.fori_loop(0, rows, inverse, 0)
-        copies = halo(z_ref, 0)
-        for copy in copies:
-            copy.start()
-        lax.fori_loop(0, rows - 2, stencil, 0)
-        for copy in copies:
-            copy.wait()
-        lax.fori_loop(rows - 2, rows, stencil, 0)
-
-        mine[...] = jnp.zeros_like(mine)
-
-        def fold(value):
-            value = jnp.sum(value.reshape(length_y // 8, 8, length_z), 0)
-            return sum(value[:, c : c + 128] for c in range(0, length_z, 128))
-
-        def dots(i, _):
-            z = z_ref[i + 1]
-            applied = mass_rate * z + w_ref[i]
-            w_ref[i] = applied
-            mine[0] = mine[0] + fold(z * res[i])
-            mine[1] = mine[1] + fold(z * applied)
-            return 0
-
-        lax.fori_loop(0, rows, dots, 0)
-        start_all(gath_copy, devices)
-        gath[me] = mine[...]
-        wait_all(gath_copy, devices)
-        total = jnp.sum(gath[...], 0)
-        gamma_next = jnp.sum(total[0], keepdims=True)
-        delta = jnp.sum(total[1], keepdims=True)
-        beta = jnp.where(step == 0, 0.0, gamma_next / gamma)
-        alpha_next = gamma_next / (delta - beta * gamma_next / alpha)
-
-        def update(i, _):
-            direction = z_ref[i + 1] + beta * dire[i]
-            image = w_ref[i] + beta * imag[i]
-            dire[i] = direction
+            block = product((yh_ref[...], yl_ref[...]), (mode_h[i], mode_l[i]))
+            zs[step, i] = product(parts_of(block), (zh_ref[...], zl_ref[...]))
+            return 0
+
+        lax.fori_loop(0, rows + 2, inverse, 0)
+        node = jnp.where(
+            step == 0, 1.0 / nodes[0], jnp.where(step == 1, 1.0 / nodes[1], 1.0 / nodes[2])
+        )
+        latest = zs.at[step]
+
+        def apply(i, _):
+            here, total = flux(latest, i)
+            image = mass_rate * here + total
             imag[i] = image
-            u_ref[i] = u_ref[i] + alpha_next * direction
-            res[i] = res[i] - alpha_next * image
-            return 0
-
-        lax.fori_loop(0, rows, update, 0)
-        return gamma_next, alpha_next
-
-    one = jnp.ones((1, 1), jnp.float32)
-    lax.fori_loop(0, ITERS, iteration, (one, one))
+            res[i] = res[i] - node * image
+            return 0
+
+        lax.fori_loop(0, rows, apply, 0)
+        return 0
+
+    lax.fori_loop(0, ITERS, iteration, 0)
+    products(ITERS - 1)
+
+    lane = lax.broadcasted_iota(jnp.int32, (1, 128), 1)
+    packed = jnp.zeros((1, 128), jnp.float32)
+    for k in range(ITERS):
+        for m in range(ITERS + 1):
+            total = jnp.sum(dots[k, m], keepdims=True)
+            packed = jnp.where(lane == k * (ITERS + 1) + m, total, packed)
+    mine[...] = packed
+    start_all(gath_copy, devices)
+    gath[me] = mine[...]
+    wait_all(gath_copy, devices)
+    total = jnp.sum(gath[...], 0)
+
+    def entry(k, m):
+        index = k * (ITERS + 1) + m
+        return total[:, index : index + 1]
+
+    lower = [[None] * ITERS for _ in range(ITERS)]
+    inverse_pivot, partial, pivots = [], [], []
+    for k in range(ITERS):
+        pivot = entry(k, k)
+        value = entry(k, ITERS)
+        for j in range(k):
+            pivot = pivot - lower[k][j] * lower[k][j] * pivots[j]
+            value = value - lower[k][j] * partial[j]
+        pivots.append(pivot)
+        usable = pivot > pivot_floor * entry(k, k)
+        inverse_pivot.append(jnp.where(usable, 1.0 / jnp.where(usable, pivot, 1.0), 0.0))
+        partial.append(value)
+        for i in range(k + 1, ITERS):
+            value = entry(i, k)
+            for j in range(k):
+                value = value - lower[i][j] * lower[k][j] * pivots[j]
+            lower[i][k] = value * inverse_pivot[k]
+    coefs = [None] * ITERS
+    for k in reversed(range(ITERS)):
+        value = partial[k] * inverse_pivot[k]
+        for i in range(k + 1, ITERS):
+            value = value - lower[i][k] * coefs[i]
+        coefs[k] = value
+
+    def finish(i, _):
+        value = v_ref[i]
+        for k in range(ITERS):
+            value = value + coefs[k] * zs[k, i + 1]
+        u_ref[i] = value
+        return 0
+
+    lax.fori_loop(0, rows, finish, 0)
 
 
 def fused(potential, recovery, stimulus, conductivity):
-    devices = lax.axis_size("px") * lax.axis_size("py")
+    count_y = lax.axis_size("py")
+    devices = lax.axis_size("px") * count_y
     rows, length_y, length_z = potential.shape
     part = length_y // devices
-    if part % 8 or length_z % 128 or conductivity.shape[1] % 8:
+    if count_y % 2 or part % 8 or length_z % 128 or conductivity.shape[1] % 8:
         return local(potential, recovery, stimulus, conductivity)
     drive = (
         excite_gain * potential * (potential - threshold) * (1.0 - potential) - potential * recovery
@@ -417,34 +537,39 @@
     tables = split(cas_table(length_y)) + split(cas_table(length_z))
     tables += tuple(
         jnp.asarray(table, jnp.float32)
-        for table in (rho, scale, rho**rows, 1.0 / (1.0 - rho ** (rows * devices)))
+        for table in (
+            rho, scale, rho**rows, rho ** (2 * rows), 1.0 / (1.0 - rho ** (rows * devices))
+        )
     )
     plane = (length_y, length_z)
     whole = (rows,) + plane
-
-    def vmem(shape):
-        return pltpu.VMEM(shape, jnp.float32)
+    half = (2, length_y // 2, length_z)
+    chips = devices // 2
+
+    def vmem(shape, dtype=jnp.float32):
+        return pltpu.VMEM(shape, dtype)
 
     dma = pltpu.SemaphoreType.DMA
     padded = (rows + 2,) + plane
-    slots = (devices, 2, part, length_z)
+    slots = (chips, 2, part, length_z)
     field = pl.pallas_call(
         kernel,
         out_shape=jax.ShapeDtypeStruct(whole, jnp.float32),
-        in_specs=[pl.BlockSpec(memory_space=pltpu.VMEM)] * 10,
+        in_specs=[pl.BlockSpec(memory_space=pltpu.VMEM)] * 11,
         out_specs=pl.BlockSpec(memory_space=pltpu.VMEM),
         scratch_shapes=[
             vmem(padded), vmem((rows + 1,) + plane), vmem(whole), vmem(whole),
-            vmem(whole), vmem(whole), vmem(whole), vmem(padded), vmem(whole),
-            vmem(whole), vmem(whole), vmem(plane),
-            vmem((2,) + plane), vmem(slots), vmem(slots), vmem((2,) + plane),
-            vmem((2, 8, 128)), vmem((devices, 2, 8, 128)),
-            dma((devices,)), dma((devices,)), dma((4,)), dma((4,)),
-            dma((devices,)), dma((devices,)), dma((devices,)), dma((devices,)),
+            vmem((ITERS,) + padded), vmem(whole), vmem(whole), vmem(whole), vmem(whole),
+            vmem(padded, jnp.bfloat16), vmem(padded, jnp.bfloat16),
+            vmem(half), vmem((2,) + half), vmem(half), vmem(slots), vmem(slots), vmem(half),
+            vmem(half), vmem((2,) + half),
+            vmem((ITERS, ITERS + 1, 8, 128)), vmem((1, 128)), vmem((devices, 1, 128)),
+            dma((count_y,)), dma((count_y,)), dma((4,)), dma((4,)), dma((2,)), dma((2,)),
+            dma((chips,)), dma((chips,)), dma((chips,)), dma((chips,)),
             dma((devices,)), dma((devices,)),
         ],
         compiler_params=pltpu.CompilerParams(
-            has_side_effects=True, vmem_limit_bytes=56 * 1024 * 1024
+            has_side_effects=True, vmem_limit_bytes=60 * 1024 * 1024
         ),
     )(v_star, conductivity, *tables)
     return (field, recovery_next)

time: 277 us -> 203 us (0.73)
  Pallas kernels: 268 us -> 193 us
    pallas_call x1, Pallas kernels: 268 us -> 193 us  [fused(): pl.pallas_call(kernel, out_shape=jax.ShapeDtypeStruct(whole, jnp.float32)...]
where the time goes in v1:
time: 203 us
  Pallas kernels  193 us (95%)
  other arithmetic  4.88 us (2%)
  local copies, waits for them, and re-layouts  3.8 us (2%)
    pallas_call x1, Pallas kernels, fused(): pl.pallas_call(kernel, out_shape=jax.ShapeDtypeStruct(whole, jnp.float32)...  193 us
    add x1, other arithmetic, fused(): recovery + time_step * rate * (-recovery - excite_gain * potential * (pot...  4.88 us

profile of v1, /device:TPU:0, one launch (start us, length us, event | category | flops | bytes accessed | tf_op | source)
XLA Modules:
  0.0 202.6 jit_solution(16585493751744247263)
XLA Ops:
  0.6 4.9 %multiply_add_fusion = (f32[8,256,256]{2,1,0:T(8,128)}, f32[8,256,256]{2,1,0:T(8,128)}) fusion(f32[8,256,256]{2,1,0:T(8,128)} %param.14, f32[8,256,256]{2,1,0:T(8,128)} %param.13, f32[8,256,256]{2,1,0:T(8,128)} %param.15), kind=kLoop, calls=%fused_computation | loop fusion | flops 11010048 | bytes 10485760 | tf_op jit(solution)/shard_map/add | solution.py:533
  5.5 0.8 jit_solution_.3.close_ref
  6.3 193.3 %shard_map.140 = f32[8,256,256]{2,1,0:T(8,128)} custom-call(f32[8,256,256]{2,1,0:T(8,128)} %get-tuple-element.3.v_ref, f32[32,64,256]{2,1,0:T(8,128)} %cond_in.1, bf16[256,256]{1,0:T(8,128)(2,1)} %constant.32.clone.yh_ref.zh_ref, bf16[256,256]{1,0:T(8,128)(2,1)} %constant.33.clone.yl_ref.zl_ref, bf16[256,256]{1,0:T(8,128)(2,1)} %constant.32.clone.yh_ref.zh_ref, ...), custom_call_target="tpu_custom_call" | custom-call | tf_op jit(solution)/shard_map/pallas_call | solution.py:555
  199.5 3.0 %copy.16 = f32[8,256,256]{2,1,0:T(8,128)} copy(f32[8,256,256]{2,1,0:T(8,128)} %shard_map.140) | data formatting | bytes 4194304

commit v2 on v1

--- a/solution.py
+++ b/solution.py
@@ -166,7 +166,7 @@
     v_ref, cond_in, yh_ref, yl_ref, zh_ref, zl_ref, rho_ref, scale_ref, sigma_ref, pair_ref,
     close_ref,
     u_ref,
-    cond, face_x, face_y, face_z, zs, res, first, imag, spec, mode_h, mode_l,
+    cond, face_x, face_y, face_z, zs, res, first, imag, spec, mode_h, mode_l, turn_h, turn_l,
     out, both_ends, chip, recv, sol, car, back, carry, dots, mine, gath,
     c_send, c_recv, h_send, h_recv, p_send, p_recv, e_send, e_recv, s_send, s_recv,
     g_send, g_recv,
@@ -206,18 +206,12 @@
         )
 
     def start_all(make, count):
-        def begin(k, _):
+        for k in range(1, count):
             make(k).start()
-            return 0
-
-        lax.fori_loop(1, count, begin, 0)
 
     def wait_all(make, count):
-        def finish(k, _):
+        for k in range(1, count):
             make(k).wait()
-            return 0
-
-        lax.fori_loop(1, count, finish, 0)
 
     def cond_copy(k):
         other = (my_y + k) % count_y
@@ -274,7 +268,8 @@
         return 0
 
     lax.fori_loop(0, rows, clear, 0)
-    wait_all(cond_copy, count_y)
+    with jax.named_scope("cond_wait"):
+        wait_all(cond_copy, count_y)
     cond_halo = halo(cond, 2)
     for copy in cond_halo:
         copy.start()
@@ -285,9 +280,10 @@
         face_z[i] = 0.5 * (here + pltpu.roll(here, length_z - 1, 1))
         return 0
 
-    lax.fori_loop(0, rows, faces, 0)
-    for copy in cond_halo + field_halo:
-        copy.wait()
+    with jax.named_scope("face_halo"):
+        lax.fori_loop(0, rows, faces, 0)
+        for copy in cond_halo + field_halo:
+            copy.wait()
 
     def faces_along(i, _):
         face_x[i] = 0.5 * (cond[i] + cond[i + 1])
@@ -301,7 +297,8 @@
         res[i] = -total
         return 0
 
-    lax.fori_loop(0, rows, begin, 0)
+    with jax.named_scope("begin"):
+        lax.fori_loop(0, rows, begin, 0)
 
     def products(step):
         block = 8
@@ -414,42 +411,82 @@
 
         lax.fori_loop(0, chips, place, (pair[0] * close, pair[1] * close), unroll=4)
 
+    def ahead_z(i, _):
+        turned = product(parts_of(res[i]), (zh_ref[...], zl_ref[...]))
+        turn_h[i], turn_l[i] = parts_of(turned)
+        return 0
+
+    def ahead_y(side):
+        at = pl.ds(pl.multiple_of(side * half, half), half)
+
+        def body(i, _):
+            spec[i, at, :] = product((yh_ref[at, :], yl_ref[at, :]), (turn_h[i], turn_l[i]))
+            return 0
+
+        lax.fori_loop(0, rows, body, 0, unroll=4)
+
+    def inverse_z(side):
+        at = pl.ds(pl.multiple_of(side * half, half), half)
+
+        def body(i, _):
+            modes = (mode_h[i, at, :], mode_l[i, at, :])
+            turn_h[i, at, :], turn_l[i, at, :] = parts_of(
+                product(modes, (zh_ref[...], zl_ref[...]))
+            )
+            return 0
+
+        lax.fori_loop(0, rows + 2, body, 0, unroll=5)
+
     def iteration(step, _):
-        def ahead(i, _):
-            block = product(parts_of(res[i]), (zh_ref[...], zl_ref[...]))
-            spec[i] = product((yh_ref[...], yl_ref[...]), parts_of(block))
-            return 0
-
-        lax.fori_loop(0, rows, ahead, 0)
-        block_ends(spec, 1 - core, out)
+        with jax.named_scope("ahead_z"):
+            lax.fori_loop(0, rows, ahead_z, 0, unroll=4)
+        with jax.named_scope("ahead_y1"):
+            ahead_y(1 - core)
+        with jax.named_scope("ends1"):
+            block_ends(spec, 1 - core, out)
         pair_ends.start()
-        block_ends(spec, core, both_ends.at[core])
-        pair_ends.wait()
+        with jax.named_scope("ahead_y2"):
+            ahead_y(core)
+        with jax.named_scope("ends2"):
+            block_ends(spec, core, both_ends.at[core])
+        with jax.named_scope("pair_wait"):
+            pair_ends.wait()
         chip_ends()
-        start_all(ends_copy, chips)
-        recv[my_chip] = chip[:, strip(my_chip), :]
+        with jax.named_scope("ends_start"):
+            start_all(ends_copy, chips)
+            recv[my_chip] = chip[:, strip(my_chip), :]
 
         @pl.when(step > 0)
         def _():
             products(step - 1)
 
-        wait_all(ends_copy, chips)
-        solve()
-        start_all(carry_copy, chips)
-        car[:, strip(my_chip), :] = sol[my_chip]
-        wait_all(carry_copy, chips)
-        core_carries()
-        pair_carry.start()
-        recur(core)
-        pair_carry.wait()
-        recur(1 - core)
+        with jax.named_scope("ends_wait"):
+            wait_all(ends_copy, chips)
+        with jax.named_scope("solve"):
+            solve()
+            start_all(carry_copy, chips)
+            car[:, strip(my_chip), :] = sol[my_chip]
+        with jax.named_scope("carry_wait"):
+            wait_all(carry_copy, chips)
+        with jax.named_scope("recur1"):
+            core_carries()
+            pair_carry.start()
+            recur(core)
+        with jax.named_scope("inverse_z1"):
+            inverse_z(core)
+        with jax.named_scope("carry_pair_wait"):
+            pair_carry.wait()
+        with jax.named_scope("recur2"):
+            recur(1 - core)
+        with jax.named_scope("inverse_z2"):
+            inverse_z(1 - core)
 
         def inverse(i, _):
-            block = product((yh_ref[...], yl_ref[...]), (mode_h[i], mode_l[i]))
-            zs[step, i] = product(parts_of(block), (zh_ref[...], zl_ref[...]))
-            return 0
-
-        lax.fori_loop(0, rows + 2, inverse, 0)
+            zs[step, i] = product((yh_ref[...], yl_ref[...]), (turn_h[i], turn_l[i]))
+            return 0
+
+        with jax.named_scope("inverse_y"):
+            lax.fori_loop(0, rows + 2, inverse, 0, unroll=5)
         node = jnp.where(
             step == 0, 1.0 / nodes[0], jnp.where(step == 1, 1.0 / nodes[1], 1.0 / nodes[2])
         )
@@ -462,11 +499,13 @@
             res[i] = res[i] - node * image
             return 0
 
-        lax.fori_loop(0, rows, apply, 0)
+        with jax.named_scope("apply"):
+            lax.fori_loop(0, rows, apply, 0)
         return 0
 
     lax.fori_loop(0, ITERS, iteration, 0)
-    products(ITERS - 1)
+    with jax.named_scope("last_products"):
+        products(ITERS - 1)
 
     lane = lax.broadcasted_iota(jnp.int32, (1, 128), 1)
     packed = jnp.zeros((1, 128), jnp.float32)
@@ -475,9 +514,10 @@
             total = jnp.sum(dots[k, m], keepdims=True)
             packed = jnp.where(lane == k * (ITERS + 1) + m, total, packed)
     mine[...] = packed
-    start_all(gath_copy, devices)
-    gath[me] = mine[...]
-    wait_all(gath_copy, devices)
+    with jax.named_scope("gather"):
+        start_all(gath_copy, devices)
+        gath[me] = mine[...]
+        wait_all(gath_copy, devices)
     total = jnp.sum(gath[...], 0)
 
     def entry(k, m):
@@ -515,7 +555,8 @@
         u_ref[i] = value
         return 0
 
-    lax.fori_loop(0, rows, finish, 0)
+    with jax.named_scope("finish"):
+        lax.fori_loop(0, rows, finish, 0)
 
 
 def fused(potential, recovery, stimulus, conductivity):
@@ -561,6 +602,7 @@
             vmem(padded), vmem((rows + 1,) + plane), vmem(whole), vmem(whole),
             vmem((ITERS,) + padded), vmem(whole), vmem(whole), vmem(whole), vmem(whole),
             vmem(padded, jnp.bfloat16), vmem(padded, jnp.bfloat16),
+            vmem(padded, jnp.bfloat16), vmem(padded, jnp.bfloat16),
             vmem(half), vmem((2,) + half), vmem(half), vmem(slots), vmem(slots), vmem(half),
             vmem(half), vmem((2,) + half),
             vmem((ITERS, ITERS + 1, 8, 128)), vmem((1, 128)), vmem((devices, 1, 128)),

time: 203 us -> 175 us (0.86)
  Pallas kernels: 193 us -> 166 us
    pallas_call x1, Pallas kernels: 193 us -> 166 us  [fused(): pl.pallas_call(kernel, out_shape=jax.ShapeDtypeStruct(whole, jnp.float32)...]
where the time goes in v2:
time: 175 us
  Pallas kernels  166 us (95%)
  other arithmetic  4.88 us (3%)
  local copies, waits for them, and re-layouts  3.8 us (2%)
    pallas_call x1, Pallas kernels, fused(): pl.pallas_call(kernel, out_shape=jax.ShapeDtypeStruct(whole, jnp.float32)...  166 us
    add x1, other arithmetic, fused(): recovery + time_step * rate * (-recovery - excite_gain * potential * (pot...  4.88 us

profile of v2, /device:TPU:0, one launch (start us, length us, event | category | flops | bytes accessed | tf_op | source)
XLA Modules:
  0.0 175.0 jit_solution(13360822699242659987)
XLA Ops:
  0.6 4.9 %multiply_add_fusion = (f32[8,256,256]{2,1,0:T(8,128)}, f32[8,256,256]{2,1,0:T(8,128)}) fusion(f32[8,256,256]{2,1,0:T(8,128)} %param.14, f32[8,256,256]{2,1,0:T(8,128)} %param.13, f32[8,256,256]{2,1,0:T(8,128)} %param.15), kind=kLoop, calls=%fused_computation | loop fusion | flops 11010048 | bytes 10485760 | tf_op jit(solution)/shard_map/add | solution.py:574
  5.5 0.8 jit_solution_.3.close_ref
  6.3 165.7 %shard_map.140 = f32[8,256,256]{2,1,0:T(8,128)} custom-call(f32[8,256,256]{2,1,0:T(8,128)} %get-tuple-element.3.v_ref, f32[32,64,256]{2,1,0:T(8,128)} %cond_in.1, bf16[256,256]{1,0:T(8,128)(2,1)} %constant.32.clone.yh_ref.zh_ref, bf16[256,256]{1,0:T(8,128)(2,1)} %constant.33.clone.yl_ref.zl_ref, bf16[256,256]{1,0:T(8,128)(2,1)} %constant.32.clone.yh_ref.zh_ref, ...), custom_call_target="tpu_custom_call" | custom-call | tf_op jit(solution)/shard_map/pallas_call | solution.py:596
  171.9 3.0 %copy.16 = f32[8,256,256]{2,1,0:T(8,128)} copy(f32[8,256,256]{2,1,0:T(8,128)} %shard_map.140) | data formatting | bytes 4194304

commit v3 on v2

--- a/solution.py
+++ b/solution.py
@@ -163,13 +163,15 @@
 
 
 def kernel(
-    v_ref, cond_in, yh_ref, yl_ref, zh_ref, zl_ref, rho_ref, scale_ref, sigma_ref, pair_ref,
-    close_ref,
+    v_hbm, w_hbm, i_hbm, cond_in, yh_in, yl_in, zh_in, zl_in, rho_in, scale_in, sigma_in,
+    pair_in, wrap_in,
     u_ref,
+    v_ref, w_ref, i_ref, yh_ref, yl_ref, zh_ref, zl_ref, rho_ref, scale_ref, sigma_ref,
+    pair_ref, wrap_ref,
     cond, face_x, face_y, face_z, zs, res, first, imag, spec, mode_h, mode_l, turn_h, turn_l,
     out, both_ends, chip, recv, sol, car, back, carry, dots, mine, gath,
     c_send, c_recv, h_send, h_recv, p_send, p_recv, e_send, e_recv, s_send, s_recv,
-    g_send, g_recv,
+    g_send, g_recv, l_sem,
 ):
     count_y = lax.axis_size("py")
     devices = lax.axis_size("px") * count_y
@@ -213,12 +215,12 @@
         for k in range(1, count):
             make(k).wait()
 
-    def cond_copy(k):
+    def cond_copy(row, k):
         other = (my_y + k) % count_y
         return pltpu.make_async_remote_copy(
-            cond_in.at[pl.ds(other * rows, rows)],
-            cond.at[pl.ds(1, rows), pl.ds(pl.multiple_of(my_y * wide_y, 8), wide_y), :],
-            c_send.at[k], c_recv.at[k],
+            cond_in.at[other * rows + row],
+            cond.at[row + 1, pl.ds(pl.multiple_of(my_y * wide_y, 8), wide_y), :],
+            c_send.at[row, k], c_recv.at[row, k],
             device_id=(lax.axis_index("px"), other), device_id_type=mesh_type,
         )
 
@@ -251,16 +253,47 @@
         flow = face_z[i] * (here - pltpu.roll(here, length_z - 1, 1))
         return here, total + (flow - pltpu.roll(flow, 1, 1))
 
-    start_all(cond_copy, count_y)
+    def local_copy(source, target, index):
+        return pltpu.make_async_copy(source, target, l_sem.at[index])
+
+    for row in (0, rows - 1) + tuple(range(1, rows - 1)):
+        for k in range(1, count_y):
+            cond_copy(row, k).start()
+    own_cond = local_copy(
+        cond_in.at[pl.ds(my_y * rows, rows)],
+        cond.at[pl.ds(1, rows), pl.ds(pl.multiple_of(my_y * wide_y, 8), wide_y), :],
+        0,
+    )
+    ionic = [
+        local_copy(source, target, 1 + n)
+        for n, (source, target) in enumerate(((v_hbm, v_ref), (w_hbm, w_ref), (i_hbm, i_ref)))
+    ]
+    loads = [
+        local_copy(source, target, 4 + n)
+        for n, (source, target) in enumerate((
+            (yh_in, yh_ref), (yl_in, yl_ref), (zh_in, zh_ref), (zl_in, zl_ref),
+            (rho_in, rho_ref), (scale_in, scale_ref), (sigma_in, sigma_ref),
+            (pair_in, pair_ref), (wrap_in, wrap_ref),
+        ))
+    ]
+    for copy in ionic + [own_cond] + loads:
+        copy.start()
+    for copy in ionic:
+        copy.wait()
     start = zs.at[0]
-    for i in range(rows):
-        start[i + 1] = v_ref[i]
+
+    def react(i, _):
+        v = v_ref[i]
+        drive = excite_gain * v * (v - threshold) * (1.0 - v) - v * w_ref[i]
+        v = v + time_step * (drive + i_ref[i])
+        v_ref[i] = v
+        start[i + 1] = v
+        return 0
+
+    lax.fori_loop(0, rows, react, 0)
     field_halo = halo(start, 0)
     for copy in field_halo:
         copy.start()
-    cond[pl.ds(1, rows), pl.ds(pl.multiple_of(my_y * wide_y, 8), wide_y), :] = cond_in[
-        pl.ds(my_y * rows, rows)
-    ]
 
     def clear(i, _):
         for k in range(1, ITERS):
@@ -268,37 +301,70 @@
         return 0
 
     lax.fori_loop(0, rows, clear, 0)
-    with jax.named_scope("cond_wait"):
-        wait_all(cond_copy, count_y)
+    own_cond.wait()
+    for copy in loads:
+        copy.wait()
+
+    def arrive(row):
+        for k in range(1, count_y):
+            cond_copy(row, k).wait_recv()
+
+    def faces(i):
+        here = cond[i + 1]
+        face_y[i] = 0.5 * (here + pltpu.roll(here, length_y - 1, 0))
+        face_z[i] = 0.5 * (here + pltpu.roll(here, length_z - 1, 1))
+
+    def faces_along(i):
+        face_x[i] = 0.5 * (cond[i] + cond[i + 1])
+
+    def begin(i):
+        _, total = flux(start, i)
+        first[i] = -total
+        res[i] = -total
+        ahead_z(i, 0)
+
+    def ahead_z(i, _):
+        turned = product(parts_of(res[i]), (zh_ref[...], zl_ref[...]))
+        turn_h[i], turn_l[i] = parts_of(turned)
+        return 0
+
+    with jax.named_scope("cond_first"):
+        arrive(0)
+        arrive(rows - 1)
     cond_halo = halo(cond, 2)
     for copy in cond_halo:
         copy.start()
-
-    def faces(i, _):
-        here = cond[i + 1]
-        face_y[i] = 0.5 * (here + pltpu.roll(here, length_y - 1, 0))
-        face_z[i] = 0.5 * (here + pltpu.roll(here, length_z - 1, 1))
+    faces(0)
+    faces(rows - 1)
+    with jax.named_scope("cond_1"):
+        arrive(1)
+    faces(1)
+    faces_along(1)
+    for copy in field_halo:
+        copy.wait()
+
+    def stream(t, _):
+        arrive(t)
+        faces(t)
+        faces_along(t)
+        begin(t - 1)
         return 0
 
-    with jax.named_scope("face_halo"):
-        lax.fori_loop(0, rows, faces, 0)
-        for copy in cond_halo + field_halo:
+    with jax.named_scope("cond_stream"):
+        lax.fori_loop(2, rows - 1, stream, 0)
+    with jax.named_scope("cond_halo"):
+        for copy in cond_halo:
             copy.wait()
-
-    def faces_along(i, _):
-        face_x[i] = 0.5 * (cond[i] + cond[i + 1])
-        return 0
-
-    lax.fori_loop(0, rows + 1, faces_along, 0)
-
-    def begin(i, _):
-        _, total = flux(start, i)
-        first[i] = -total
-        res[i] = -total
-        return 0
-
-    with jax.named_scope("begin"):
-        lax.fori_loop(0, rows, begin, 0)
+    with jax.named_scope("cond_tail"):
+        faces_along(rows - 1)
+        faces_along(0)
+        faces_along(rows)
+        begin(rows - 2)
+        begin(0)
+        begin(rows - 1)
+        for row in range(rows):
+            for k in range(1, count_y):
+                cond_copy(row, k).wait_send()
 
     def products(step):
         block = 8
@@ -393,7 +459,7 @@
     def solve():
         own = pl.ds(pl.multiple_of(core * half + my_chip * part, part), part)
         sigma = pair_ref[own, :]
-        close = close_ref[own, :]
+        close = 1.0 / (1.0 - wrap_ref[own, :])
         zero = jnp.zeros_like(sigma)
 
         def sums(b, pair):
@@ -411,11 +477,6 @@
 
         lax.fori_loop(0, chips, place, (pair[0] * close, pair[1] * close), unroll=4)
 
-    def ahead_z(i, _):
-        turned = product(parts_of(res[i]), (zh_ref[...], zl_ref[...]))
-        turn_h[i], turn_l[i] = parts_of(turned)
-        return 0
-
     def ahead_y(side):
         at = pl.ds(pl.multiple_of(side * half, half), half)
 
@@ -438,8 +499,11 @@
         lax.fori_loop(0, rows + 2, body, 0, unroll=5)
 
     def iteration(step, _):
-        with jax.named_scope("ahead_z"):
-            lax.fori_loop(0, rows, ahead_z, 0, unroll=4)
+        @pl.when(step > 0)
+        def _():
+            with jax.named_scope("ahead_z"):
+                lax.fori_loop(0, rows, ahead_z, 0, unroll=4)
+
         with jax.named_scope("ahead_y1"):
             ahead_y(1 - core)
         with jax.named_scope("ends1"):
@@ -566,10 +630,6 @@
     part = length_y // devices
     if count_y % 2 or part % 8 or length_z % 128 or conductivity.shape[1] % 8:
         return local(potential, recovery, stimulus, conductivity)
-    drive = (
-        excite_gain * potential * (potential - threshold) * (1.0 - potential) - potential * recovery
-    )
-    v_star = potential + time_step * (drive + stimulus)
     rate = base_rate + rate_slope * recovery / (potential + rate_shift)
     recovery_next = recovery + time_step * rate * (
         -recovery - excite_gain * potential * (potential - threshold - 1.0)
@@ -579,7 +639,7 @@
     tables += tuple(
         jnp.asarray(table, jnp.float32)
         for table in (
-            rho, scale, rho**rows, rho ** (2 * rows), 1.0 / (1.0 - rho ** (rows * devices))
+            rho, scale, rho**rows, rho ** (2 * rows), rho ** (rows * devices)
         )
     )
     plane = (length_y, length_z)
@@ -592,13 +652,16 @@
 
     dma = pltpu.SemaphoreType.DMA
     padded = (rows + 2,) + plane
+    square = [vmem((n, n), jnp.bfloat16) for n in (length_y, length_y, length_z, length_z)]
     slots = (chips, 2, part, length_z)
     field = pl.pallas_call(
         kernel,
         out_shape=jax.ShapeDtypeStruct(whole, jnp.float32),
-        in_specs=[pl.BlockSpec(memory_space=pltpu.VMEM)] * 11,
+        in_specs=[pl.BlockSpec(memory_space=pl.ANY)] * 13,
         out_specs=pl.BlockSpec(memory_space=pltpu.VMEM),
         scratch_shapes=[
+            vmem(whole), vmem(whole), vmem(whole), *square,
+            *(vmem(plane) for _ in range(5)),
             vmem(padded), vmem((rows + 1,) + plane), vmem(whole), vmem(whole),
             vmem((ITERS,) + padded), vmem(whole), vmem(whole), vmem(whole), vmem(whole),
             vmem(padded, jnp.bfloat16), vmem(padded, jnp.bfloat16),
@@ -606,14 +669,14 @@
             vmem(half), vmem((2,) + half), vmem(half), vmem(slots), vmem(slots), vmem(half),
             vmem(half), vmem((2,) + half),
             vmem((ITERS, ITERS + 1, 8, 128)), vmem((1, 128)), vmem((devices, 1, 128)),
-            dma((count_y,)), dma((count_y,)), dma((4,)), dma((4,)), dma((2,)), dma((2,)),
+            dma((rows, count_y)), dma((rows, count_y)), dma((4,)), dma((4,)), dma((2,)), dma((2,)),
             dma((chips,)), dma((chips,)), dma((chips,)), dma((chips,)),
-            dma((devices,)), dma((devices,)),
+            dma((devices,)), dma((devices,)), dma((13,)),
         ],
         compiler_params=pltpu.CompilerParams(
             has_side_effects=True, vmem_limit_bytes=60 * 1024 * 1024
         ),
-    )(v_star, conductivity, *tables)
+    )(potential, recovery, stimulus, conductivity, *tables)
     return (field, recovery_next)
 
 

time: 175 us -> 168 us (0.960)
  Pallas kernels: 166 us -> 162 us
  local copies, waits for them, and re-layouts: 3.8 us -> 1.33 us
    pallas_call x1, Pallas kernels: 166 us -> 162 us  [fused(): pl.pallas_call(kernel, out_shape=jax.ShapeDtypeStruct(whole, jnp.float32)...]
where the time goes in v3:
time: 168 us
  Pallas kernels  162 us (96%)
  other arithmetic  3.94 us (2%)
    pallas_call x1, Pallas kernels, fused(): pl.pallas_call(kernel, out_shape=jax.ShapeDtypeStruct(whole, jnp.float32)...  162 us
    add x1, other arithmetic, fused(): recovery + time_step * rate * (-recovery - excite_gain * potential * (pot...  3.94 us

profile of v3, /device:TPU:0, one launch (start us, length us, event | category | flops | bytes accessed | tf_op | source)
XLA Modules:
  0.0 167.6 jit_solution(128266758099160080)
XLA Ops:
  0.6 0.0 copy-start
  0.6 161.7 %shard_map.140 = f32[8,256,256]{2,1,0:T(8,128)} custom-call(f32[8,256,256]{2,1,0:T(8,128)} %v_hbm.1, f32[8,256,256]{2,1,0:T(8,128)} %w_hbm.1, f32[8,256,256]{2,1,0:T(8,128)} %i_hbm.1, f32[32,64,256]{2,1,0:T(8,128)} %cond_in.1, bf16[256,256]{1,0:T(8,128)(2,1)} %constant.30.clone.yh_in.zh_in, bf16[256,256]{1,0:T(8,128)(2,1)} %constant.31.clone.yl_in.zl_in, ...), custom_call_target="tpu_custom_call" | custom-call | tf_op jit(solution)/shard_map/pallas_call | solution.py:657
  162.3 0.0 copy-done
  162.3 0.0 copy-start.1
  162.4 3.9 %multiply_add_fusion = f32[8,256,256]{2,1,0:T(8,128)} fusion(f32[8,256,256]{2,1,0:T(8,128)} %w_hbm.1, f32[8,256,256]{2,1,0:T(8,128)S(1)} %copy-done), kind=kLoop, calls=%fused_computation | loop fusion | flops 6291456 | bytes 6291456 | tf_op jit(solution)/shard_map/add | solution.py:634
  166.3 0.0 copy-done.1
  166.3 1.3 copy.16
Async XLA Ops:
  0.6 161.7 %copy-start = (f32[8,256,256]{2,1,0:T(8,128)S(1)}, f32[8,256,256]{2,1,0:T(8,128)}, u32[]{:S(2)}) copy-start(f32[8,256,256]{2,1,0:T(8,128)} %v_hbm.1) | copy-start | bytes 6291460
  162.3 4.0 %copy-start.1 = (f32[8,256,256]{2,1,0:T(8,128)S(1)}, f32[8,256,256]{2,1,0:T(8,128)}, u32[]{:S(2)}) copy-start(f32[8,256,256]{2,1,0:T(8,128)} %shard_map.140) | copy-start | bytes 6291460

commit v4 on v3

--- a/solution.py
+++ b/solution.py
@@ -18,6 +18,7 @@
 rate_shift = 0.3
 time_step = 0.1
 nodes = (2.6, 1.0, 4.0)
+BLOCK = 64
 pivot_floor = 1e-6
 AXES = ("px", "py")
 
@@ -144,6 +145,10 @@
     return (field, recovery_next)
 
 
+def bits(count):
+    return [1 << n for n in range(count.bit_length() - 1)]
+
+
 def split(table):
     high = table.astype(jnp.bfloat16)
     low = (table - high.astype(np.float64)).astype(jnp.bfloat16)
@@ -171,7 +176,7 @@
     cond, face_x, face_y, face_z, zs, res, first, imag, spec, mode_h, mode_l, turn_h, turn_l,
     out, both_ends, chip, recv, sol, car, back, carry, dots, mine, gath,
     c_send, c_recv, h_send, h_recv, p_send, p_recv, e_send, e_recv, s_send, s_recv,
-    g_send, g_recv, l_sem,
+    g_send, g_recv, l_sem, r_sem,
 ):
     count_y = lax.axis_size("py")
     devices = lax.axis_size("px") * count_y
@@ -245,20 +250,43 @@
     pair_ends = remote(out, both_ends.at[core], p_send.at[0], p_recv.at[0], partner)
     pair_carry = remote(back, carry.at[core], p_send.at[1], p_recv.at[1], partner)
 
-    def flux(field, i):
-        here = field[i + 1]
-        total = face_x[i + 1] * (here - field[i + 2]) - face_x[i] * (field[i] - here)
-        flow = face_y[i] * (here - pltpu.roll(here, length_y - 1, 0))
-        total = total + (flow - pltpu.roll(flow, 1, 0))
-        flow = face_z[i] * (here - pltpu.roll(here, length_z - 1, 1))
-        return here, total + (flow - pltpu.roll(flow, 1, 1))
+    def flux(field, i, low, block):
+        at = slice(low, low + block)
+        before = slice((low - 8) % length_y, (low - 8) % length_y + 8)
+        after = slice((low + block) % length_y, (low + block) % length_y + 8)
+        here = field[i + 1, at]
+        total = face_x[i + 1, at] * (here - field[i + 2, at]) - face_x[i, at] * (
+            field[i, at] - here
+        )
+        wide = jnp.concatenate([field[i + 1, before], here, field[i + 1, after]], 0)
+        drop = wide - pltpu.roll(wide, block + 15, 0)
+        flow = jnp.concatenate([face_y[i, before], face_y[i, at]], 0) * drop[: block + 8]
+        total = total + (flow[8:] - pltpu.roll(flow, 1, 0)[8:])
+        flow = face_z[i, at] * (here - pltpu.roll(here, length_z - 1, 1))
+        return at, here, total + (flow - pltpu.roll(flow, 1, 1))
+
+    def row_blocks(block):
+        return range(0, length_y, block)
 
     def local_copy(source, target, index):
         return pltpu.make_async_copy(source, target, l_sem.at[index])
 
-    for row in (0, rows - 1) + tuple(range(1, rows - 1)):
-        for k in range(1, count_y):
-            cond_copy(row, k).start()
+    my_x = lax.axis_index("px")
+    size_x = lax.axis_size("px")
+    rounds = [(my_x + bit - 2 * bit * (my_x // bit % 2)) * count_y + my_y for bit in bits(size_x)]
+    greeted = [my_x * count_y + (my_y + k) % count_y for k in range(1, count_y)] + rounds
+    barrier = pltpu.get_barrier_semaphore()
+    for other in greeted:
+        pl.semaphore_signal(barrier, 1, device_id=device(other), device_id_type=mesh_type)
+    pl.semaphore_wait(barrier, len(greeted))
+
+    def tell(n):
+        pl.semaphore_signal(r_sem.at[n], 1, device_id=device(rounds[n]), device_id_type=mesh_type)
+
+    with jax.named_scope("issue"):
+        for row in (0, rows - 1) + tuple(range(1, rows - 1)):
+            for k in range(1, count_y):
+                cond_copy(row, k).start()
     own_cond = local_copy(
         cond_in.at[pl.ds(my_y * rows, rows)],
         cond.at[pl.ds(1, rows), pl.ds(pl.multiple_of(my_y * wide_y, 8), wide_y), :],
@@ -276,10 +304,15 @@
             (pair_in, pair_ref), (wrap_in, wrap_ref),
         ))
     ]
-    for copy in ionic + [own_cond] + loads:
-        copy.start()
-    for copy in ionic:
-        copy.wait()
+    with jax.named_scope("issue_local"):
+        for copy in ionic + [own_cond] + loads:
+            copy.start()
+    with jax.named_scope("ionic_wait"):
+        for copy in ionic:
+            copy.wait()
+    for n in range(len(rounds)):
+        tell(n)
+        pl.semaphore_wait(r_sem.at[n], 1)
     start = zs.at[0]
 
     def react(i, _):
@@ -301,9 +334,10 @@
         return 0
 
     lax.fori_loop(0, rows, clear, 0)
-    own_cond.wait()
-    for copy in loads:
-        copy.wait()
+    with jax.named_scope("loads_wait"):
+        own_cond.wait()
+        for copy in loads:
+            copy.wait()
 
     def arrive(row):
         for k in range(1, count_y):
@@ -318,9 +352,10 @@
         face_x[i] = 0.5 * (cond[i] + cond[i + 1])
 
     def begin(i):
-        _, total = flux(start, i)
-        first[i] = -total
-        res[i] = -total
+        for low in row_blocks(BLOCK):
+            at, _, total = flux(start, i, low, BLOCK)
+            first[i, at] = -total
+            res[i, at] = -total
         ahead_z(i, 0)
 
     def ahead_z(i, _):
@@ -381,7 +416,10 @@
             return tuple(sums)
 
         zero = jnp.zeros((block, length_z), jnp.float32)
-        sums = lax.fori_loop(0, rows * per, body, (zero,) * (ITERS + 1), unroll=4)
+        sums = lax.fori_loop(0, rows * per, body, (zero,) * (ITERS + 1), unroll=16)
+        keep(step, sums)
+
+    def keep(step, sums):
         for m, total in enumerate(sums):
             dots[step, m] = sum(total[:, c : c + 128] for c in range(0, length_z, 128))
 
@@ -557,20 +595,38 @@
         latest = zs.at[step]
 
         def apply(i, _):
-            here, total = flux(latest, i)
-            image = mass_rate * here + total
-            imag[i] = image
-            res[i] = res[i] - node * image
+            for low in row_blocks(BLOCK):
+                at, here, total = flux(latest, i, low, BLOCK)
+                image = mass_rate * here + total
+                imag[i, at] = image
+                res[i, at] = res[i, at] - node * image
             return 0
 
-        with jax.named_scope("apply"):
-            lax.fori_loop(0, rows, apply, 0)
+        def folded(value):
+            return jnp.sum(value.reshape(value.shape[0] // 8, 8, length_z), 0)
+
+        def apply_last(i, sums):
+            for low in row_blocks(BLOCK):
+                at, here, total = flux(latest, i, low, BLOCK)
+                image = mass_rate * here + total
+                fresh = [zs[j, i + 1, at] * image for j in range(ITERS)] + [here * first[i, at]]
+                sums = tuple(old + folded(new) for old, new in zip(sums, fresh))
+            return sums
+
+        @pl.when(step < ITERS - 1)
+        def _():
+            with jax.named_scope("apply"):
+                lax.fori_loop(0, rows, apply, 0)
+
+        @pl.when(step == ITERS - 1)
+        def _():
+            with jax.named_scope("apply_last"):
+                zero = jnp.zeros((8, length_z), jnp.float32)
+                keep(step, lax.fori_loop(0, rows, apply_last, (zero,) * (ITERS + 1)))
+
         return 0
 
     lax.fori_loop(0, ITERS, iteration, 0)
-    with jax.named_scope("last_products"):
-        products(ITERS - 1)
-
     lane = lax.broadcasted_iota(jnp.int32, (1, 128), 1)
     packed = jnp.zeros((1, 128), jnp.float32)
     for k in range(ITERS):
@@ -613,10 +669,12 @@
         coefs[k] = value
 
     def finish(i, _):
-        value = v_ref[i]
-        for k in range(ITERS):
-            value = value + coefs[k] * zs[k, i + 1]
-        u_ref[i] = value
+        for low in row_blocks(BLOCK):
+            at = slice(low, low + BLOCK)
+            value = v_ref[i, at]
+            for k in range(ITERS):
+                value = value + coefs[k] * zs[k, i + 1, at]
+            u_ref[i, at] = value
         return 0
 
     with jax.named_scope("finish"):
@@ -628,7 +686,8 @@
     devices = lax.axis_size("px") * count_y
     rows, length_y, length_z = potential.shape
     part = length_y // devices
-    if count_y % 2 or part % 8 or length_z % 128 or conductivity.shape[1] % 8:
+    size_x = lax.axis_size("px")
+    if size_x & (size_x - 1) or count_y % 2 or part % 8 or length_z % 128 or conductivity.shape[1] % 8:
         return local(potential, recovery, stimulus, conductivity)
     rate = base_rate + rate_slope * recovery / (potential + rate_shift)
     recovery_next = recovery + time_step * rate * (
@@ -672,9 +731,10 @@
             dma((rows, count_y)), dma((rows, count_y)), dma((4,)), dma((4,)), dma((2,)), dma((2,)),
             dma((chips,)), dma((chips,)), dma((chips,)), dma((chips,)),
             dma((devices,)), dma((devices,)), dma((13,)),
+            pltpu.SemaphoreType.REGULAR((len(bits(size_x)),)),
         ],
         compiler_params=pltpu.CompilerParams(
-            has_side_effects=True, vmem_limit_bytes=60 * 1024 * 1024
+            collective_id=0, has_side_effects=True, vmem_limit_bytes=60 * 1024 * 1024
         ),
     )(potential, recovery, stimulus, conductivity, *tables)
     return (field, recovery_next)

time: 168 us -> 161 us (0.958)
  Pallas kernels: 162 us -> 154 us
    pallas_call x1, Pallas kernels: 162 us -> 154 us  [fused(): pl.pallas_call(kernel, out_shape=jax.ShapeDtypeStruct(whole, jnp.float32)...]
where the time goes in v4:
time: 161 us; the launch traced here: 160 us
  Pallas kernels  154 us (96%)
  other arithmetic  3.94 us (2%)
    pallas_call x1, Pallas kernels, fused(): pl.pallas_call(kernel, out_shape=jax.ShapeDtypeStruct(whole, jnp.float32)...  154 us
    add x1, other arithmetic, fused(): recovery + time_step * rate * (-recovery - excite_gain * potential * (pot...  3.94 us

profile of v4, /device:TPU:0, one launch (start us, length us, event | category | flops | bytes accessed | tf_op | source)
XLA Modules:
  0.0 160.4 jit_solution(289767881365527795)
XLA Ops:
  0.6 0.0 copy-start
  0.6 154.5 %shard_map.140 = f32[8,256,256]{2,1,0:T(8,128)} custom-call(f32[8,256,256]{2,1,0:T(8,128)} %v_hbm.1, f32[8,256,256]{2,1,0:T(8,128)} %w_hbm.1, f32[8,256,256]{2,1,0:T(8,128)} %i_hbm.1, f32[32,64,256]{2,1,0:T(8,128)} %cond_in.1, bf16[256,256]{1,0:T(8,128)(2,1)} %constant.30.clone.yh_in.zh_in, bf16[256,256]{1,0:T(8,128)(2,1)} %constant.31.clone.yl_in.zl_in, ...), custom_call_target="tpu_custom_call" | custom-call | tf_op jit(solution)/shard_map/pallas_call | solution.py:716
  155.1 0.0 copy-done
  155.1 0.0 copy-start.1
  155.1 3.9 %multiply_add_fusion = f32[8,256,256]{2,1,0:T(8,128)} fusion(f32[8,256,256]{2,1,0:T(8,128)} %w_hbm.1, f32[8,256,256]{2,1,0:T(8,128)S(1)} %copy-done), kind=kLoop, calls=%fused_computation | loop fusion | flops 6291456 | bytes 6291456 | tf_op jit(solution)/shard_map/add | solution.py:693
  159.1 0.0 copy-done.1
  159.1 1.3 copy.16
Async XLA Ops:
  0.6 154.5 %copy-start = (f32[8,256,256]{2,1,0:T(8,128)S(1)}, f32[8,256,256]{2,1,0:T(8,128)}, u32[]{:S(2)}) copy-start(f32[8,256,256]{2,1,0:T(8,128)} %v_hbm.1) | copy-start | bytes 6291460
  155.1 4.0 %copy-start.1 = (f32[8,256,256]{2,1,0:T(8,128)S(1)}, f32[8,256,256]{2,1,0:T(8,128)}, u32[]{:S(2)}) copy-start(f32[8,256,256]{2,1,0:T(8,128)} %shard_map.140) | copy-start | bytes 6291460

commit v5 on v4

--- a/solution.py
+++ b/solution.py
@@ -188,11 +188,22 @@
     rows, length_y, length_z = v_ref.shape
     half = length_y // 2
     part = half // chips
+    quarter = half // 2
+    owners = chips // 2
     wide_y = cond_in.shape[1]
     mesh_type = pl.DeviceIdType.MESH
 
     def device(index):
         return (index // count_y, index % count_y)
+
+    def tint(index):
+        return (index // 2 + index // 4) % 2
+
+    def owner(chunk, index):
+        return 2 * index + (chunk + tint(2 * index)) % 2
+
+    my_chunk = (my_chip + tint(my_chip)) % 2
+    my_strip = my_chunk * owners + my_chip // 2
 
     def strip(index):
         return pl.ds(pl.multiple_of(index * part, part), part)
@@ -229,26 +240,59 @@
             device_id=(lax.axis_index("px"), other), device_id_type=mesh_type,
         )
 
-    def ends_copy(k):
-        other = (my_chip + k) % chips
+    def ends_copy(chunk, index, source):
+        at = chunk * owners + index
         return remote(
-            chip.at[:, strip(other), :], recv.at[my_chip], e_send.at[k], e_recv.at[k],
+            chip.at[:, strip(at), :], recv.at[source], e_send.at[at], e_recv.at[source],
+            2 * owner(chunk, index) + core,
+        )
+
+    def carry_copy(other, source, strip_at):
+        return remote(
+            sol.at[other], car.at[:, strip(strip_at), :], s_send.at[other], s_recv.at[source],
             2 * other + core,
         )
 
-    def carry_copy(k):
-        other = (my_chip + k) % chips
-        return remote(
-            sol.at[other], car.at[:, strip(my_chip), :], s_send.at[k], s_recv.at[k],
-            2 * other + core,
-        )
+    def unless_mine(other, action):
+        pl.when(other != my_chip)(action)
+
+    def ends_start(chunk):
+        for index in range(owners):
+            index = (my_chip // 2 + index) % owners
+            unless_mine(owner(chunk, index), ends_copy(chunk, index, my_chip).start)
+
+    def ends_wait():
+        for chunk in range(2):
+            for index in range(owners):
+                unless_mine(owner(chunk, index), ends_copy(chunk, index, my_chip).wait_send)
+        for source in range(chips):
+            unless_mine(source, ends_copy(0, 0, source).wait_recv)
+
+    def carry_start():
+        for k in range(1, chips):
+            carry_copy((my_chip + k) % chips, my_chip, my_strip).start()
+
+    def carry_wait(chunk):
+        for index in range(owners):
+            other = owner(chunk, index)
+            unless_mine(other, carry_copy(0, other, chunk * owners + index).wait_recv)
+
+    def carry_sent():
+        for k in range(1, chips):
+            carry_copy((my_chip + k) % chips, my_chip, my_strip).wait_send()
 
     def gath_copy(k):
         return remote(mine, gath.at[me], g_send.at[k], g_recv.at[k], (me + k) % devices)
 
     partner = me + 1 - 2 * core
     pair_ends = remote(out, both_ends.at[core], p_send.at[0], p_recv.at[0], partner)
-    pair_carry = remote(back, carry.at[core], p_send.at[1], p_recv.at[1], partner)
+    pair_carry = []
+    for n in range(2):
+        cut = pl.ds(n * quarter, quarter)
+        pair_carry.append(remote(
+            back.at[:, cut, :], carry.at[core, :, cut, :], p_send.at[1 + n], p_recv.at[1 + n],
+            partner,
+        ))
 
     def flux(field, i, low, block):
         at = slice(low, low + block)
@@ -439,20 +483,20 @@
 
         lax.fori_loop(0, half // block, body, 0, unroll=2)
 
-    def chip_ends(block=8):
+    def chip_ends(chunk, block=8):
         def body(b, _):
-            low = pl.multiple_of(b * block, block)
+            low = pl.multiple_of(chunk * quarter + b * block, block)
             at = pl.ds(low, block)
             sigma = sigma_ref[pl.ds(pl.multiple_of(core * half + low, block), block), :]
             chip[0, at, :] = both_ends[1, 0, at, :] + sigma * both_ends[0, 0, at, :]
             chip[1, at, :] = both_ends[0, 1, at, :] + sigma * both_ends[1, 1, at, :]
             return 0
 
-        lax.fori_loop(0, half // block, body, 0, unroll=4)
-
-    def core_carries(block=8):
+        lax.fori_loop(0, quarter // block, body, 0, unroll=4)
+
+    def core_carries(chunk, block=8):
         def body(b, _):
-            low = pl.multiple_of(b * block, block)
+            low = pl.multiple_of(chunk * quarter + b * block, block)
             at = pl.ds(low, block)
             sigma = sigma_ref[pl.ds(pl.multiple_of(core * half + low, block), block), :]
             left, right = car[0, at, :], car[1, at, :]
@@ -464,11 +508,11 @@
             back[1, at, :] = jnp.where(core == 0, right, after)
             return 0
 
-        lax.fori_loop(0, half // block, body, 0, unroll=4)
-
-    def recur(side, block=16, wide=128):
+        lax.fori_loop(0, quarter // block, body, 0, unroll=4)
+
+    def recur(side, chunk, block=16, wide=128):
         def body(b, _):
-            low = pl.multiple_of(b * block, block)
+            low = pl.multiple_of(chunk * quarter + b * block, block)
             at = pl.ds(pl.multiple_of(side * half + low, block), block)
             for c in range(0, length_z, wide):
                 cut = slice(c, c + wide)
@@ -492,10 +536,10 @@
                     mode_h[i, at, cut], mode_l[i, at, cut] = parts_of(scale * mode)
             return 0
 
-        lax.fori_loop(0, half // block, body, 0)
+        lax.fori_loop(0, quarter // block, body, 0)
 
     def solve():
-        own = pl.ds(pl.multiple_of(core * half + my_chip * part, part), part)
+        own = pl.ds(pl.multiple_of(core * half + my_strip * part, part), part)
         sigma = pair_ref[own, :]
         close = 1.0 / (1.0 - wrap_ref[own, :])
         zero = jnp.zeros_like(sigma)
@@ -524,17 +568,23 @@
 
         lax.fori_loop(0, rows, body, 0, unroll=4)
 
-    def inverse_z(side):
-        at = pl.ds(pl.multiple_of(side * half, half), half)
-
-        def body(i, _):
-            modes = (mode_h[i, at, :], mode_l[i, at, :])
-            turn_h[i, at, :], turn_l[i, at, :] = parts_of(
-                product(modes, (zh_ref[...], zl_ref[...]))
+    def inverse_z(side, chunk):
+        at = pl.ds(pl.multiple_of(side * half + chunk * quarter, quarter), quarter)
+
+        group = (rows + 2) // 2
+
+        def body(g, _):
+            planes = pl.ds(g * group, group)
+            shape = (group, quarter, length_z)
+            modes = tuple(
+                mode[planes, at, :].reshape(group * quarter, length_z) for mode in (mode_h, mode_l)
             )
+            high, low = parts_of(product(modes, (zh_ref[...], zl_ref[...])))
+            turn_h[planes, at, :] = high.reshape(shape)
+            turn_l[planes, at, :] = low.reshape(shape)
             return 0
 
-        lax.fori_loop(0, rows + 2, body, 0, unroll=5)
+        lax.fori_loop(0, 2, body, 0, unroll=True)
 
     def iteration(step, _):
         @pl.when(step > 0)
@@ -553,35 +603,41 @@
             block_ends(spec, core, both_ends.at[core])
         with jax.named_scope("pair_wait"):
             pair_ends.wait()
-        chip_ends()
         with jax.named_scope("ends_start"):
-            start_all(ends_copy, chips)
-            recv[my_chip] = chip[:, strip(my_chip), :]
+            chip_ends(0)
+            ends_start(0)
+            chip_ends(1)
 
         @pl.when(step > 0)
         def _():
             products(step - 1)
 
+        with jax.named_scope("ends_start1"):
+            ends_start(1)
+            recv[my_chip] = chip[:, strip(my_strip), :]
+
         with jax.named_scope("ends_wait"):
-            wait_all(ends_copy, chips)
+            ends_wait()
         with jax.named_scope("solve"):
             solve()
-            start_all(carry_copy, chips)
-            car[:, strip(my_chip), :] = sol[my_chip]
-        with jax.named_scope("carry_wait"):
-            wait_all(carry_copy, chips)
-        with jax.named_scope("recur1"):
-            core_carries()
-            pair_carry.start()
-            recur(core)
-        with jax.named_scope("inverse_z1"):
-            inverse_z(core)
-        with jax.named_scope("carry_pair_wait"):
-            pair_carry.wait()
-        with jax.named_scope("recur2"):
-            recur(1 - core)
-        with jax.named_scope("inverse_z2"):
-            inverse_z(1 - core)
+            carry_start()
+            car[:, strip(my_strip), :] = sol[my_chip]
+        for chunk in range(2):
+            with jax.named_scope("carry_wait"):
+                carry_wait(chunk)
+            with jax.named_scope("recur1"):
+                core_carries(chunk)
+                pair_carry[chunk].start()
+                recur(core, chunk)
+            with jax.named_scope("inverse_z1"):
+                inverse_z(core, chunk)
+            with jax.named_scope("carry_pair_wait"):
+                pair_carry[chunk].wait()
+            with jax.named_scope("recur2"):
+                recur(1 - core, chunk)
+            with jax.named_scope("inverse_z2"):
+                inverse_z(1 - core, chunk)
+        carry_sent()
 
         def inverse(i, _):
             zs[step, i] = product((yh_ref[...], yl_ref[...]), (turn_h[i], turn_l[i]))
@@ -687,7 +743,7 @@
     rows, length_y, length_z = potential.shape
     part = length_y // devices
     size_x = lax.axis_size("px")
-    if size_x & (size_x - 1) or count_y % 2 or part % 8 or length_z % 128 or conductivity.shape[1] % 8:
+    if size_x & (size_x - 1) or size_x < 2 or count_y % 2 or part % 8 or length_z % 128 or conductivity.shape[1] % 8:
         return local(potential, recovery, stimulus, conductivity)
     rate = base_rate + rate_slope * recovery / (potential + rate_shift)
     recovery_next = recovery + time_step * rate * (
@@ -728,7 +784,7 @@
             vmem(half), vmem((2,) + half), vmem(half), vmem(slots), vmem(slots), vmem(half),
             vmem(half), vmem((2,) + half),
             vmem((ITERS, ITERS + 1, 8, 128)), vmem((1, 128)), vmem((devices, 1, 128)),
-            dma((rows, count_y)), dma((rows, count_y)), dma((4,)), dma((4,)), dma((2,)), dma((2,)),
+            dma((rows, count_y)), dma((rows, count_y)), dma((4,)), dma((4,)), dma((3,)), dma((3,)),
             dma((chips,)), dma((chips,)), dma((chips,)), dma((chips,)),
             dma((devices,)), dma((devices,)), dma((13,)),
             pltpu.SemaphoreType.REGULAR((len(bits(size_x)),)),

time: 161 us -> 157 us (0.975)
  Pallas kernels: 154 us -> 151 us
    pallas_call x1, Pallas kernels: 154 us -> 151 us  [fused(): pl.pallas_call(kernel, out_shape=jax.ShapeDtypeStruct(whole, jnp.float32)...]
where the time goes in v5:
time: 157 us
  Pallas kernels  151 us (96%)
  other arithmetic  3.94 us (3%)
    pallas_call x1, Pallas kernels, fused(): pl.pallas_call(kernel, out_shape=jax.ShapeDtypeStruct(whole, jnp.float32)...  151 us
    add x1, other arithmetic, fused(): recovery + time_step * rate * (-recovery - excite_gain * potential * (pot...  3.94 us

profile of v5, /device:TPU:0, one launch (start us, length us, event | category | flops | bytes accessed | tf_op | source)
XLA Modules:
  0.0 156.8 jit_solution(14531680221913119335)
XLA Ops:
  0.6 0.0 copy-start
  0.6 150.9 %shard_map.140 = f32[8,256,256]{2,1,0:T(8,128)} custom-call(f32[8,256,256]{2,1,0:T(8,128)} %v_hbm.1, f32[8,256,256]{2,1,0:T(8,128)} %w_hbm.1, f32[8,256,256]{2,1,0:T(8,128)} %i_hbm.1, f32[32,64,256]{2,1,0:T(8,128)} %cond_in.1, bf16[256,256]{1,0:T(8,128)(2,1)} %constant.30.clone.yh_in.zh_in, bf16[256,256]{1,0:T(8,128)(2,1)} %constant.31.clone.yl_in.zl_in, ...), custom_call_target="tpu_custom_call" | custom-call | tf_op jit(solution)/shard_map/pallas_call | solution.py:772
  151.5 0.0 copy-done
  151.5 0.0 copy-start.1
  151.5 3.9 %multiply_add_fusion = f32[8,256,256]{2,1,0:T(8,128)} fusion(f32[8,256,256]{2,1,0:T(8,128)} %w_hbm.1, f32[8,256,256]{2,1,0:T(8,128)S(1)} %copy-done), kind=kLoop, calls=%fused_computation | loop fusion | flops 6291456 | bytes 6291456 | tf_op jit(solution)/shard_map/add | solution.py:749
  155.5 0.0 copy-done.1
  155.5 1.3 copy.16
Async XLA Ops:
  0.6 150.9 %copy-start = (f32[8,256,256]{2,1,0:T(8,128)S(1)}, f32[8,256,256]{2,1,0:T(8,128)}, u32[]{:S(2)}) copy-start(f32[8,256,256]{2,1,0:T(8,128)} %v_hbm.1) | copy-start | bytes 6291460
  151.5 4.0 %copy-start.1 = (f32[8,256,256]{2,1,0:T(8,128)S(1)}, f32[8,256,256]{2,1,0:T(8,128)}, u32[]{:S(2)}) copy-start(f32[8,256,256]{2,1,0:T(8,128)} %shard_map.140) | copy-start | bytes 6291460

commit v6 on v5

--- a/solution.py
+++ b/solution.py
@@ -170,13 +170,13 @@
 def kernel(
     v_hbm, w_hbm, i_hbm, cond_in, yh_in, yl_in, zh_in, zl_in, rho_in, scale_in, sigma_in,
     pair_in, wrap_in,
-    u_ref,
+    u_hbm,
     v_ref, w_ref, i_ref, yh_ref, yl_ref, zh_ref, zl_ref, rho_ref, scale_ref, sigma_ref,
     pair_ref, wrap_ref,
-    cond, face_x, face_y, face_z, zs, res, first, imag, spec, mode_h, mode_l, turn_h, turn_l,
+    cond, face_x, face_y, face_z, back_y, back_z, centre, zs, res, first, imag, spec, mode_h, mode_l, turn_h, turn_l,
     out, both_ends, chip, recv, sol, car, back, carry, dots, mine, gath,
     c_send, c_recv, h_send, h_recv, p_send, p_recv, e_send, e_recv, s_send, s_recv,
-    g_send, g_recv, l_sem, r_sem,
+    g_send, g_recv, l_sem, r_sem, u_sem, k_send, k_recv,
 ):
     count_y = lax.axis_size("py")
     devices = lax.axis_size("px") * count_y
@@ -299,15 +299,16 @@
         before = slice((low - 8) % length_y, (low - 8) % length_y + 8)
         after = slice((low + block) % length_y, (low + block) % length_y + 8)
         here = field[i + 1, at]
-        total = face_x[i + 1, at] * (here - field[i + 2, at]) - face_x[i, at] * (
-            field[i, at] - here
-        )
         wide = jnp.concatenate([field[i + 1, before], here, field[i + 1, after]], 0)
-        drop = wide - pltpu.roll(wide, block + 15, 0)
-        flow = jnp.concatenate([face_y[i, before], face_y[i, at]], 0) * drop[: block + 8]
-        total = total + (flow[8:] - pltpu.roll(flow, 1, 0)[8:])
-        flow = face_z[i, at] * (here - pltpu.roll(here, length_z - 1, 1))
-        return at, here, total + (flow - pltpu.roll(flow, 1, 1))
+        count = block + 16
+        image = centre[i, at] * here
+        image = image - face_x[i + 1, at] * field[i + 2, at]
+        image = image - face_x[i, at] * field[i, at]
+        image = image - face_y[i, at] * pltpu.roll(wide, count - 1, 0)[8 : block + 8]
+        image = image - back_y[i, at] * pltpu.roll(wide, 1, 0)[8 : block + 8]
+        image = image - face_z[i, at] * pltpu.roll(here, length_z - 1, 1)
+        image = image - back_z[i, at] * pltpu.roll(here, 1, 1)
+        return at, here, image
 
     def row_blocks(block):
         return range(0, length_y, block)
@@ -320,9 +321,10 @@
     rounds = [(my_x + bit - 2 * bit * (my_x // bit % 2)) * count_y + my_y for bit in bits(size_x)]
     greeted = [my_x * count_y + (my_y + k) % count_y for k in range(1, count_y)] + rounds
     barrier = pltpu.get_barrier_semaphore()
-    for other in greeted:
-        pl.semaphore_signal(barrier, 1, device_id=device(other), device_id_type=mesh_type)
-    pl.semaphore_wait(barrier, len(greeted))
+    with jax.named_scope("greet"):
+        for other in greeted:
+            pl.semaphore_signal(barrier, 1, device_id=device(other), device_id_type=mesh_type)
+        pl.semaphore_wait(barrier, len(greeted))
 
     def tell(n):
         pl.semaphore_signal(r_sem.at[n], 1, device_id=device(rounds[n]), device_id_type=mesh_type)
@@ -390,37 +392,70 @@
     def faces(i):
         here = cond[i + 1]
         face_y[i] = 0.5 * (here + pltpu.roll(here, length_y - 1, 0))
+        back_y[i] = 0.5 * (here + pltpu.roll(here, 1, 0))
         face_z[i] = 0.5 * (here + pltpu.roll(here, length_z - 1, 1))
+        back_z[i] = 0.5 * (here + pltpu.roll(here, 1, 1))
 
     def faces_along(i):
         face_x[i] = 0.5 * (cond[i] + cond[i + 1])
 
     def begin(i):
         for low in row_blocks(BLOCK):
-            at, _, total = flux(start, i, low, BLOCK)
-            first[i, at] = -total
-            res[i, at] = -total
+            at = slice(low, low + BLOCK)
+            centre[i, at] = (
+                mass_rate
+                + (face_x[i, at] + face_x[i + 1, at])
+                + (face_y[i, at] + back_y[i, at])
+                + (face_z[i, at] + back_z[i, at])
+            )
+            _, here, image = flux(start, i, low, BLOCK)
+            value = mass_rate * here - image
+            first[i, at] = value
+            res[i, at] = value
         ahead_z(i, 0)
+        spec[i] = product((yh_ref[...], yl_ref[...]), (turn_h[i], turn_l[i]))
 
     def ahead_z(i, _):
         turned = product(parts_of(res[i]), (zh_ref[...], zl_ref[...]))
         turn_h[i], turn_l[i] = parts_of(turned)
         return 0
 
+    def edge_copy(m, slot_row):
+        row = 2 * rows * m + (2 * rows - 1) * (1 - slot_row)
+        target = (my_x * count_y + 2 * m + 2 - 3 * slot_row + devices) % devices
+        at = pl.ds(pl.multiple_of(my_y * wide_y, 8), wide_y)
+        place = cond.at[slot_row * (rows + 1), at, :]
+        here = local_copy(cond_in.at[row], place, 13)
+        there = remote(
+            cond_in.at[row], place, k_send.at[2 * m + slot_row], k_recv.at[my_y], target
+        )
+        return target, here, there
+
+    def edge_arrival(k):
+        place = cond.at[core * (rows + 1), pl.ds(k * wide_y, wide_y), :]
+        return remote(cond_in.at[0], place, k_send.at[0], k_recv.at[k], partner)
+
+    edges = [(m, side) for m in range(count_y // 2) for side in range(2)]
+    for m, side in edges:
+        target, here, there = edge_copy(m, side)
+        pl.when(target == me)(here.start)
+        pl.when(target != me)(there.start)
+    owner_x = ((me + 2 * core - 1 + devices) % devices) // count_y
+
     with jax.named_scope("cond_first"):
         arrive(0)
         arrive(rows - 1)
-    cond_halo = halo(cond, 2)
-    for copy in cond_halo:
-        copy.start()
+    inner = remote(
+        cond.at[rows - core * (rows - 1)], cond.at[core * (rows + 1)],
+        h_send.at[2], h_recv.at[2], partner,
+    )
+    inner.start()
     faces(0)
     faces(rows - 1)
     with jax.named_scope("cond_1"):
         arrive(1)
     faces(1)
     faces_along(1)
-    for copy in field_halo:
-        copy.wait()
 
     def stream(t, _):
         arrive(t)
@@ -431,14 +466,21 @@
 
     with jax.named_scope("cond_stream"):
         lax.fori_loop(2, rows - 1, stream, 0)
+    faces_along(rows - 1)
+    begin(rows - 2)
     with jax.named_scope("cond_halo"):
-        for copy in cond_halo:
+        for copy in field_halo:
             copy.wait()
+        inner.wait()
+        for m, side in edges:
+            target, here, there = edge_copy(m, side)
+            pl.when(target == me)(here.wait)
+            pl.when(target != me)(there.wait_send)
+        for k in range(count_y):
+            pl.when(owner_x * count_y + k != me)(edge_arrival(k).wait_recv)
     with jax.named_scope("cond_tail"):
-        faces_along(rows - 1)
         faces_along(0)
         faces_along(rows)
-        begin(rows - 2)
         begin(0)
         begin(rows - 1)
         for row in range(rows):
@@ -592,13 +634,20 @@
             with jax.named_scope("ahead_z"):
                 lax.fori_loop(0, rows, ahead_z, 0, unroll=4)
 
-        with jax.named_scope("ahead_y1"):
-            ahead_y(1 - core)
+        @pl.when(step > 0)
+        def _():
+            with jax.named_scope("ahead_y1"):
+                ahead_y(1 - core)
+
         with jax.named_scope("ends1"):
             block_ends(spec, 1 - core, out)
         pair_ends.start()
-        with jax.named_scope("ahead_y2"):
-            ahead_y(core)
+
+        @pl.when(step > 0)
+        def _():
+            with jax.named_scope("ahead_y2"):
+                ahead_y(core)
+
         with jax.named_scope("ends2"):
             block_ends(spec, core, both_ends.at[core])
         with jax.named_scope("pair_wait"):
@@ -652,8 +701,7 @@
 
         def apply(i, _):
             for low in row_blocks(BLOCK):
-                at, here, total = flux(latest, i, low, BLOCK)
-                image = mass_rate * here + total
+                at, here, image = flux(latest, i, low, BLOCK)
                 imag[i, at] = image
                 res[i, at] = res[i, at] - node * image
             return 0
@@ -663,8 +711,7 @@
 
         def apply_last(i, sums):
             for low in row_blocks(BLOCK):
-                at, here, total = flux(latest, i, low, BLOCK)
-                image = mass_rate * here + total
+                at, here, image = flux(latest, i, low, BLOCK)
                 fresh = [zs[j, i + 1, at] * image for j in range(ITERS)] + [here * first[i, at]]
                 sums = tuple(old + folded(new) for old, new in zip(sums, fresh))
             return sums
@@ -724,17 +771,23 @@
             value = value - lower[i][k] * coefs[i]
         coefs[k] = value
 
+    def result(i):
+        return pltpu.make_async_copy(v_ref.at[i], u_hbm.at[i], u_sem.at[i])
+
     def finish(i, _):
         for low in row_blocks(BLOCK):
             at = slice(low, low + BLOCK)
             value = v_ref[i, at]
             for k in range(ITERS):
                 value = value + coefs[k] * zs[k, i + 1, at]
-            u_ref[i, at] = value
+            v_ref[i, at] = value
+        result(i).start()
         return 0
 
     with jax.named_scope("finish"):
         lax.fori_loop(0, rows, finish, 0)
+        for i in range(rows):
+            result(i).wait()
 
 
 def fused(potential, recovery, stimulus, conductivity):
@@ -773,11 +826,11 @@
         kernel,
         out_shape=jax.ShapeDtypeStruct(whole, jnp.float32),
         in_specs=[pl.BlockSpec(memory_space=pl.ANY)] * 13,
-        out_specs=pl.BlockSpec(memory_space=pltpu.VMEM),
+        out_specs=pl.BlockSpec(memory_space=pl.ANY),
         scratch_shapes=[
             vmem(whole), vmem(whole), vmem(whole), *square,
             *(vmem(plane) for _ in range(5)),
-            vmem(padded), vmem((rows + 1,) + plane), vmem(whole), vmem(whole),
+            vmem(padded), vmem((rows + 1,) + plane), *(vmem(whole) for _ in range(5)),
             vmem((ITERS,) + padded), vmem(whole), vmem(whole), vmem(whole), vmem(whole),
             vmem(padded, jnp.bfloat16), vmem(padded, jnp.bfloat16),
             vmem(padded, jnp.bfloat16), vmem(padded, jnp.bfloat16),
@@ -786,8 +839,9 @@
             vmem((ITERS, ITERS + 1, 8, 128)), vmem((1, 128)), vmem((devices, 1, 128)),
             dma((rows, count_y)), dma((rows, count_y)), dma((4,)), dma((4,)), dma((3,)), dma((3,)),
             dma((chips,)), dma((chips,)), dma((chips,)), dma((chips,)),
-            dma((devices,)), dma((devices,)), dma((13,)),
+            dma((devices,)), dma((devices,)), dma((14,)),
             pltpu.SemaphoreType.REGULAR((len(bits(size_x)),)),
+            dma((rows,)), dma((count_y,)), dma((count_y,)),
         ],
         compiler_params=pltpu.CompilerParams(
             collective_id=0, has_side_effects=True, vmem_limit_bytes=60 * 1024 * 1024

time: 157 us -> 150 us (0.955)
  Pallas kernels: 151 us -> 143 us
    pallas_call x1, Pallas kernels: 151 us -> 143 us  [fused(): pl.pallas_call(kernel, out_shape=jax.ShapeDtypeStruct(whole, jnp.float32)...]
where the time goes in v6:
time: 150 us; the launch traced here: 149 us
  Pallas kernels  143 us (95%)
  other arithmetic  3.94 us (3%)
    pallas_call x1, Pallas kernels, fused(): pl.pallas_call(kernel, out_shape=jax.ShapeDtypeStruct(whole, jnp.float32)...  143 us
    add x1, other arithmetic, fused(): recovery + time_step * rate * (-recovery - excite_gain * potential * (pot...  3.94 us

profile of v6, /device:TPU:0, one launch (start us, length us, event | category | flops | bytes accessed | tf_op | source)
XLA Modules:
  0.0 149.4 jit_solution(5654369590844496020)
XLA Ops:
  0.6 0.0 copy-start
  0.6 143.4 %shard_map.140 = f32[8,256,256]{2,1,0:T(8,128)} custom-call(f32[8,256,256]{2,1,0:T(8,128)} %v_hbm.1, f32[8,256,256]{2,1,0:T(8,128)} %w_hbm.1, f32[8,256,256]{2,1,0:T(8,128)} %i_hbm.1, f32[32,64,256]{2,1,0:T(8,128)} %cond_in.1, bf16[256,256]{1,0:T(8,128)(2,1)} %constant.30.clone.yh_in.zh_in, bf16[256,256]{1,0:T(8,128)(2,1)} %constant.31.clone.yl_in.zl_in, ...), custom_call_target="tpu_custom_call" | custom-call | tf_op jit(solution)/shard_map/pallas_call | solution.py:825
  144.1 0.0 copy-done
  144.1 0.0 copy-start.1
  144.1 3.9 %multiply_add_fusion = f32[8,256,256]{2,1,0:T(8,128)} fusion(f32[8,256,256]{2,1,0:T(8,128)} %w_hbm.1, f32[8,256,256]{2,1,0:T(8,128)S(1)} %copy-done), kind=kLoop, calls=%fused_computation | loop fusion | flops 6291456 | bytes 6291456 | tf_op jit(solution)/shard_map/add | solution.py:802
  148.1 0.0 copy-done.1
  148.1 1.3 copy.16
Async XLA Ops:
  0.6 143.5 %copy-start = (f32[8,256,256]{2,1,0:T(8,128)S(1)}, f32[8,256,256]{2,1,0:T(8,128)}, u32[]{:S(2)}) copy-start(f32[8,256,256]{2,1,0:T(8,128)} %v_hbm.1) | copy-start | bytes 6291460
  144.1 4.0 %copy-start.1 = (f32[8,256,256]{2,1,0:T(8,128)S(1)}, f32[8,256,256]{2,1,0:T(8,128)}, u32[]{:S(2)}) copy-start(f32[8,256,256]{2,1,0:T(8,128)} %shard_map.140) | copy-start | bytes 6291460

commit v7 on v6

--- a/solution.py
+++ b/solution.py
@@ -170,7 +170,7 @@
 def kernel(
     v_hbm, w_hbm, i_hbm, cond_in, yh_in, yl_in, zh_in, zl_in, rho_in, scale_in, sigma_in,
     pair_in, wrap_in,
-    u_hbm,
+    u_hbm, n_hbm,
     v_ref, w_ref, i_ref, yh_ref, yl_ref, zh_ref, zl_ref, rho_ref, scale_ref, sigma_ref,
     pair_ref, wrap_ref,
     cond, face_x, face_y, face_z, back_y, back_z, centre, zs, res, first, imag, spec, mode_h, mode_l, turn_h, turn_l,
@@ -262,11 +262,13 @@
             unless_mine(owner(chunk, index), ends_copy(chunk, index, my_chip).start)
 
     def ends_wait():
+        for source in range(chips):
+            unless_mine(source, ends_copy(0, 0, source).wait_recv)
+
+    def ends_sent():
         for chunk in range(2):
             for index in range(owners):
                 unless_mine(owner(chunk, index), ends_copy(chunk, index, my_chip).wait_send)
-        for source in range(chips):
-            unless_mine(source, ends_copy(0, 0, source).wait_recv)
 
     def carry_start():
         for k in range(1, chips):
@@ -362,14 +364,18 @@
     start = zs.at[0]
 
     def react(i, _):
-        v = v_ref[i]
-        drive = excite_gain * v * (v - threshold) * (1.0 - v) - v * w_ref[i]
+        v, w = v_ref[i], w_ref[i]
+        rate = base_rate + rate_slope * w / (v + rate_shift)
+        w_ref[i] = w + time_step * rate * (-w - excite_gain * v * (v - threshold - 1.0))
+        drive = excite_gain * v * (v - threshold) * (1.0 - v) - v * w
         v = v + time_step * (drive + i_ref[i])
         v_ref[i] = v
         start[i + 1] = v
         return 0
 
     lax.fori_loop(0, rows, react, 0)
+    recovered = pltpu.make_async_copy(w_ref, n_hbm, u_sem.at[rows])
+    recovered.start()
     field_halo = halo(start, 0)
     for copy in field_halo:
         copy.start()
@@ -523,7 +529,7 @@
             target[1, pl.ds(low, block), :] = tail
             return 0
 
-        lax.fori_loop(0, half // block, body, 0, unroll=2)
+        lax.fori_loop(0, half // block, body, 0, unroll=4)
 
     def chip_ends(chunk, block=8):
         def body(b, _):
@@ -608,7 +614,7 @@
             spec[i, at, :] = product((yh_ref[at, :], yl_ref[at, :]), (turn_h[i], turn_l[i]))
             return 0
 
-        lax.fori_loop(0, rows, body, 0, unroll=4)
+        lax.fori_loop(0, rows, body, 0, unroll=8)
 
     def inverse_z(side, chunk):
         at = pl.ds(pl.multiple_of(side * half + chunk * quarter, quarter), quarter)
@@ -632,7 +638,7 @@
         @pl.when(step > 0)
         def _():
             with jax.named_scope("ahead_z"):
-                lax.fori_loop(0, rows, ahead_z, 0, unroll=4)
+                lax.fori_loop(0, rows, ahead_z, 0, unroll=8)
 
         @pl.when(step > 0)
         def _():
@@ -686,6 +692,7 @@
                 recur(1 - core, chunk)
             with jax.named_scope("inverse_z2"):
                 inverse_z(1 - core, chunk)
+        ends_sent()
         carry_sent()
 
         def inverse(i, _):
@@ -693,7 +700,7 @@
             return 0
 
         with jax.named_scope("inverse_y"):
-            lax.fori_loop(0, rows + 2, inverse, 0, unroll=5)
+            lax.fori_loop(0, rows + 2, inverse, 0, unroll=10)
         node = jnp.where(
             step == 0, 1.0 / nodes[0], jnp.where(step == 1, 1.0 / nodes[1], 1.0 / nodes[2])
         )
@@ -788,6 +795,7 @@
         lax.fori_loop(0, rows, finish, 0)
         for i in range(rows):
             result(i).wait()
+        recovered.wait()
 
 
 def fused(potential, recovery, stimulus, conductivity):
@@ -798,10 +806,6 @@
     size_x = lax.axis_size("px")
     if size_x & (size_x - 1) or size_x < 2 or count_y % 2 or part % 8 or length_z % 128 or conductivity.shape[1] % 8:
         return local(potential, recovery, stimulus, conductivity)
-    rate = base_rate + rate_slope * recovery / (potential + rate_shift)
-    recovery_next = recovery + time_step * rate * (
-        -recovery - excite_gain * potential * (potential - threshold - 1.0)
-    )
     rho, scale = mode_tables(length_y, length_z)
     tables = split(cas_table(length_y)) + split(cas_table(length_z))
     tables += tuple(
@@ -822,11 +826,11 @@
     padded = (rows + 2,) + plane
     square = [vmem((n, n), jnp.bfloat16) for n in (length_y, length_y, length_z, length_z)]
     slots = (chips, 2, part, length_z)
-    field = pl.pallas_call(
+    return pl.pallas_call(
         kernel,
-        out_shape=jax.ShapeDtypeStruct(whole, jnp.float32),
+        out_shape=(jax.ShapeDtypeStruct(whole, jnp.float32),) * 2,
         in_specs=[pl.BlockSpec(memory_space=pl.ANY)] * 13,
-        out_specs=pl.BlockSpec(memory_space=pl.ANY),
+        out_specs=(pl.BlockSpec(memory_space=pl.ANY),) * 2,
         scratch_shapes=[
             vmem(whole), vmem(whole), vmem(whole), *square,
             *(vmem(plane) for _ in range(5)),
@@ -841,13 +845,12 @@
             dma((chips,)), dma((chips,)), dma((chips,)), dma((chips,)),
             dma((devices,)), dma((devices,)), dma((14,)),
             pltpu.SemaphoreType.REGULAR((len(bits(size_x)),)),
-            dma((rows,)), dma((count_y,)), dma((count_y,)),
+            dma((rows + 1,)), dma((count_y,)), dma((count_y,)),
         ],
         compiler_params=pltpu.CompilerParams(
             collective_id=0, has_side_effects=True, vmem_limit_bytes=60 * 1024 * 1024
         ),
     )(potential, recovery, stimulus, conductivity, *tables)
-    return (field, recovery_next)
 
 
 def solution(mesh):

time: 150 us -> 147 us (0.980)
  other arithmetic: 3.94 us -> 0 us
  local copies, waits for them, and re-layouts: 1.33 us -> 4.52 us
  Pallas kernels: 143 us -> 141 us
    add x1 -> x0, other arithmetic: 3.94 us -> none  [fused(): recovery + time_step * rate * (-recovery - excite_gain * potential * (pot...]
    unnamed x5 -> x4, local copies, waits for them, and re-layouts: 1.33 us -> 4.52 us
    pallas_call x1, Pallas kernels: 143 us -> 141 us  [fused(): pl.pallas_call(kernel, out_shape=(jax.ShapeDtypeStruct(whole, jnp.float32...]
where the time goes in v7:
time: 147 us
  Pallas kernels  141 us (96%)
  local copies, waits for them, and re-layouts  4.52 us (3%)
    pallas_call x1, Pallas kernels, fused(): pl.pallas_call(kernel, out_shape=(jax.ShapeDtypeStruct(whole, jnp.float32...  141 us
    unnamed x4, local copies, waits for them, and re-layouts  4.52 us

profile of v7, /device:TPU:0, one launch (start us, length us, event | category | flops | bytes accessed | tf_op | source)
XLA Modules:
  0.0 146.6 jit_solution(1683834446552667790)
XLA Ops:
  0.6 141.4 %shard_map.140 = (f32[8,256,256]{2,1,0:T(8,128)}, f32[8,256,256]{2,1,0:T(8,128)}) custom-call(f32[8,256,256]{2,1,0:T(8,128)} %v_hbm.1, f32[8,256,256]{2,1,0:T(8,128)} %w_hbm.1, f32[8,256,256]{2,1,0:T(8,128)} %i_hbm.1, f32[32,64,256]{2,1,0:T(8,128)} %cond_in.1, bf16[256,256]{1,0:T(8,128)(2,1)} %constant.14.clone.yh_in.zh_in, ...), custom_call_target="tpu_custom_call" | custom-call | tf_op jit(solution)/shard_map/pallas_call | solution.py:829
  142.1 0.0 copy-start
  142.1 3.2 %copy.17 = f32[8,256,256]{2,1,0:T(8,128)} copy(f32[8,256,256]{2,1,0:T(8,128)} %get-tuple-element.4) | data formatting | bytes 4194304
  145.3 0.0 copy-done
  145.3 1.3 copy.18
Async XLA Ops:
  142.1 3.2 %copy-start = (f32[8,256,256]{2,1,0:T(8,128)S(1)}, f32[8,256,256]{2,1,0:T(8,128)}, u32[]{:S(2)}) copy-start(f32[8,256,256]{2,1,0:T(8,128)} %get-tuple-element.5) | copy-start | bytes 6291460
